TPU v7x, 512 devices: a whole 4x4x16 slice. The times are simulated.
512 devices in a mesh: col: 64 (over y, z), inner: 2 (over core), outer: 4 (over x).
Axes of the slice: x: 4, y: 4, z: 16, core: 2. Of those that a mesh axis runs over, the one named last changes fastest.
Arguments:
- matrix: float32 [8192, 8192], P(('inner', 'outer'), 'col'), may hold values from -6 to 6
- sketch: float32 [8192, 256], P('col'), may hold values from -6 to 6
Outputs:
- basis: float32 [8192, 256], P(('inner', 'outer'))
- coeffs: float32 [256, 8192], P(None, 'col')
All inputs are finite; a program needn't handle non-finite values.
Results may differ from a plain program's by a relative error of at most 0.0006.
Values sent between devices are 32-bit elements; how exact they have to be, the bound alone decides.
No kernel may reach another device: no remote copies, remote signals or barrier semaphores. Data moves between devices by JAX's collectives and lax.ppermute only.
A program may use at most 64 MiB of HBM per device.

v0:
```python
import jax
import jax.numpy as jnp
from jax import lax
from jax.sharding import PartitionSpec as P

M = 8192


def copy_for_each(array, axis):
    length = lax.axis_size(axis)
    return lax.all_to_all(
        jnp.broadcast_to(array[None], (length, *array.shape)), axis, 0, 0, tiled=True
    )


def over_copies(array, axis):
    everything = copy_for_each(array, axis)
    return jnp.sum(everything, axis=0)


def split_up(array, dim, length):
    before, after = (array.shape[:dim], array.shape[dim + 1 :])
    return jnp.moveaxis(array.reshape(*before, length, -1, *after), dim, 0)


def summed_on_arrival(array, axis, dim):
    tiles = split_up(array, dim, lax.axis_size(axis))
    arrived = lax.all_to_all(tiles, axis, split_axis=0, concat_axis=0, tiled=True)
    return arrived.sum(axis=0)


def rows_for(lines, length):
    spare = -len(lines) % length
    return jnp.pad(lines, [(0, spare)] + [(0, 0)] * (lines.ndim - 1))


def joined_along(tiles, dim):
    tiles = jnp.moveaxis(tiles, 0, dim)
    shape = tiles.shape
    return tiles.reshape(*shape[:dim], shape[dim] * shape[dim + 1], *shape[dim + 2 :])


def gather_directly(array, axis, dim):
    return joined_along(copy_for_each(array, axis), dim)


def total_of(array, axes):
    lines = array.reshape(-1, array.shape[-1])
    own = summed_on_arrival(rows_for(lines, lax.axis_size(axes)), axes, 0)
    whole = gather_directly(own, axes, 0)
    return whole[: len(lines)].reshape(array.shape)


def product(left, right):
    return jnp.dot(left, right, precision=lax.Precision.HIGHEST, preferred_element_type=jnp.float32)


def gram_of(sample):
    return lax.dot_general(
        sample,
        sample,
        (((0,), (0,)), ((), ())),
        precision=lax.Precision.HIGHEST,
        preferred_element_type=jnp.float32,
    )


def upper_factor(gram):
    return jnp.linalg.cholesky(gram).T


def apply_inverse(sample, upper):
    solved = jax.scipy.linalg.solve_triangular(upper.T, sample.T, lower=True)
    return solved.T


def tall_factor(sample):
    gram = over_copies(gram_of(sample), ("inner", "outer"))
    upper = upper_factor(gram)
    return apply_inverse(sample, upper)


def basis_from(matrix, right):
    sample = total_of(product(matrix, right), "col")
    return tall_factor(sample)


def projected(basis_local, matrix):
    partial_proj = lax.dot_general(
        basis_local,
        matrix,
        (((0,), (0,)), ((), ())),
        precision=lax.Precision.HIGHEST,
        preferred_element_type=jnp.float32,
    )
    return over_copies(partial_proj, ("inner", "outer"))


def per_device(matrix, sketch):
    right = sketch
    basis_local = None
    projection = None
    for sweep in range(2):
        basis_local = basis_from(matrix, right)
        projection = projected(basis_local, matrix)
        right = projection.T
    scale = lax.rsqrt(jnp.mean(projection * projection, axis=0, keepdims=True) + 1e-06)
    return (basis_local * jnp.sqrt(jnp.float32(M)), projection * scale)


def solution(mesh):
    return jax.shard_map(
        per_device,
        mesh=mesh,
        in_specs=(P(("inner", "outer"), "col"), P("col", None)),
        out_specs=(P(("inner", "outer"), None), P(None, "col")),
        check_vma=False,
    )
```

profile of v0, /device:TPU:1, one launch (start us, length us, event | category | flops | bytes accessed | tf_op | source)
XLA Modules:
  0.0 498.1 jit_solution(16117011542094310576)
XLA Ops:
  1.7 2.8 fusion.29
  4.5 19.3 %all-to-all-start = ((f32[64,16,256]{2,1,0:T(8,128)}), f32[64,16,256]{2,1,0:T(8,128)S(1)}, u32[]{:S(2)}, u32[]{:S(2)}) async-start(f32[64,16,256]{2,1,0:T(8,128)} %bitcast), calls=%async_computation | async-start | bytes 2097152 | tf_op jit(solution)/shard_map/all_to_all | solution.py:28
  23.8 50.4 %all-to-all-done = f32[64,16,256]{2,1,0:T(8,128)S(1)} async-done(((f32[64,16,256]{2,1,0:T(8,128)}), f32[64,16,256]{2,1,0:T(8,128)S(1)}, u32[]{:S(2)}, u32[]{:S(2)}) %all-to-all-start) | async-done | bytes 1048608 | tf_op jit(solution)/shard_map/all_to_all | solution.py:28
  74.4 60.3 %all_to_all.40 = f32[64,16,256]{2,1,0:T(8,128)S(1)} all-to-all(f32[64,16,256]{2,1,0:T(8,128)S(1)} %broadcast_in_dim.13), channel_id=1, replica_groups=mesh['col'=64,'inner'=2,'outer'=4] {'col'}, dimensions={0} | all-to-all | bytes 2097152 | tf_op jit(solution)/shard_map/all_to_all | solution.py:11
  135.7 1.8 convolution_bitcast_fusion.2
  137.5 1.5 broadcast_in_dim.14
  139.0 8.9 %all-to-all-start.2 = ((f32[8,256,256]{2,1,0:T(8,128)}), f32[8,256,256]{2,1,0:T(8,128)S(1)}, u32[]{:S(2)}, u32[]{:S(2)}) async-start(f32[8,256,256]{2,1,0:T(8,128)} %broadcast_in_dim.14), calls=%async_computation.2 | async-start | bytes 4194304 | tf_op jit(solution)/shard_map/all_to_all | solution.py:11
  148.0 2.5 copy.24
  150.5 23.6 %all-to-all-done.2 = f32[8,256,256]{2,1,0:T(8,128)S(1)} async-done(((f32[8,256,256]{2,1,0:T(8,128)}), f32[8,256,256]{2,1,0:T(8,128)S(1)}, u32[]{:S(2)}, u32[]{:S(2)}) %all-to-all-start.2) | async-done | bytes 2097184 | tf_op jit(solution)/shard_map/all_to_all | solution.py:11
  174.5 11.7 %cholesky.130 = f32[128,128]{1,0:T(8,128)S(1)} custom-call(f32[128,128]{1,0:T(8,128)S(1)} %cholesky.194), custom_call_target="Cholesky" | custom-call | tf_op jit(solution)/shard_map/jit(cholesky)/cholesky | solution.py:69
  186.3 9.8 %custom-call.13 = f32[1,128,128]{1,2,0:T(8,128)S(1)} custom-call(f32[1,128,128]{2,1,0:T(8,128)S(1)} %get-tuple-element.55), custom_call_target="InvertDiagBlocksLowerTriangular" | custom-call | tf_op jit(solution)/shard_map/jit(cholesky)/cholesky | solution.py:69
  196.6 11.7 %cholesky.147 = f32[128,128]{1,0:T(8,128)S(1)} custom-call(f32[128,128]{1,0:T(8,128)S(1)} %convolution_subtract_fusion.3), custom_call_target="Cholesky" | custom-call | tf_op jit(solution)/shard_map/jit(cholesky)/cholesky | solution.py:69
  210.5 4.1 while.4
  211.1 1.4 bitcast_dynamic-update-slice_fusion.4
  213.2 1.4 bitcast_dynamic-update-slice_fusion.4
  214.6 19.9 %custom-call.14 = f32[2,128,128]{1,2,0:T(8,128)S(1)} custom-call(f32[2,128,128]{2,1,0:T(8,128)S(1)} %get-tuple-element.18), custom_call_target="InvertDiagBlocksLowerTriangular" | custom-call | tf_op jit(solution)/shard_map/jit(_solve_triangular)/triangular_solve | solution.py:73
  237.5 18.1 %all_to_all.42 = f32[8,256,128]{2,1,0:T(8,128)S(1)} all-to-all(f32[8,256,128]{2,1,0:T(8,128)S(1)} %broadcast_in_dim.15), channel_id=1, replica_groups=mesh['col'=64,'inner'=2,'outer'=4] {'inner','outer'}, dimensions={0} | all-to-all | bytes 2097152 | tf_op jit(solution)/shard_map/all_to_all | solution.py:11
  257.0 56.7 %all_to_all.43 = f32[64,16,256]{2,1,0:T(8,128)S(1)} all-to-all(f32[64,16,256]{2,1,0:T(8,128)S(1)} %bitcast.92), channel_id=1, replica_groups=mesh['col'=64,'inner'=2,'outer'=4] {'col'}, dimensions={0} | all-to-all | bytes 2097152 | tf_op jit(solution)/shard_map/all_to_all | solution.py:28
  314.0 60.5 %all_to_all.41 = f32[64,16,256]{2,1,0:T(8,128)S(1)} all-to-all(f32[64,16,256]{2,1,0:T(8,128)S(1)} %broadcast_in_dim.16), channel_id=1, replica_groups=mesh['col'=64,'inner'=2,'outer'=4] {'col'}, dimensions={0} | all-to-all | bytes 2097152 | tf_op jit(solution)/shard_map/all_to_all | solution.py:11
  375.4 1.8 convolution_bitcast_fusion.1
  377.3 1.5 broadcast_in_dim.17
  378.8 8.5 %all-to-all-start.6 = ((f32[8,256,256]{2,1,0:T(8,128)}), f32[8,256,256]{2,1,0:T(8,128)S(1)}, u32[]{:S(2)}, u32[]{:S(2)}) async-start(f32[8,256,256]{2,1,0:T(8,128)} %broadcast_in_dim.17), calls=%async_computation.6 | async-start | bytes 4194304 | tf_op jit(solution)/shard_map/all_to_all | solution.py:11
  387.3 2.5 copy.27
  389.8 23.6 %all-to-all-done.6 = f32[8,256,256]{2,1,0:T(8,128)S(1)} async-done(((f32[8,256,256]{2,1,0:T(8,128)}), f32[8,256,256]{2,1,0:T(8,128)S(1)}, u32[]{:S(2)}, u32[]{:S(2)}) %all-to-all-start.6) | async-done | bytes 2097184 | tf_op jit(solution)/shard_map/all_to_all | solution.py:11
  413.8 11.7 %cholesky.164 = f32[128,128]{1,0:T(8,128)S(1)} custom-call(f32[128,128]{1,0:T(8,128)S(1)} %cholesky.197), custom_call_target="Cholesky" | custom-call | tf_op jit(solution)/shard_map/jit(cholesky)/cholesky | solution.py:69
  425.6 9.8 %custom-call.15 = f32[1,128,128]{1,2,0:T(8,128)S(1)} custom-call(f32[1,128,128]{2,1,0:T(8,128)S(1)} %get-tuple-element.51), custom_call_target="InvertDiagBlocksLowerTriangular" | custom-call | tf_op jit(solution)/shard_map/jit(cholesky)/cholesky | solution.py:69
  435.9 11.7 %cholesky.181 = f32[128,128]{1,0:T(8,128)S(1)} custom-call(f32[128,128]{1,0:T(8,128)S(1)} %convolution_subtract_fusion.2), custom_call_target="Cholesky" | custom-call | tf_op jit(solution)/shard_map/jit(cholesky)/cholesky | solution.py:69
  450.4 4.1 while.5
  454.5 19.8 %custom-call.16 = f32[2,128,128]{1,2,0:T(8,128)S(1)} custom-call(f32[2,128,128]{2,1,0:T(8,128)S(1)} %get-tuple-element.19), custom_call_target="InvertDiagBlocksLowerTriangular" | custom-call | tf_op jit(solution)/shard_map/jit(_solve_triangular)/triangular_solve | solution.py:73
  478.3 3.8 all-to-all-start.7
  483.2 2.5 copy.28
  485.8 11.3 %all-to-all-done.7 = f32[8,256,128]{2,1,0:T(8,128)S(1)} async-done(((f32[8,256,128]{2,1,0:T(8,128)}), f32[8,256,128]{2,1,0:T(8,128)S(1)}, u32[]{:S(2)}, u32[]{:S(2)}) %all-to-all-start.7) | async-done | bytes 1048608 | tf_op jit(solution)/shard_map/all_to_all | solution.py:11
  (69 shorter events, 22.8 us)
Async XLA Ops:
  0.6 1.0 copy-start
  4.5 69.7 %all-to-all-start = ((f32[64,16,256]{2,1,0:T(8,128)}), f32[64,16,256]{2,1,0:T(8,128)S(1)}, u32[]{:S(2)}, u32[]{:S(2)}) async-start(f32[64,16,256]{2,1,0:T(8,128)} %bitcast), calls=%async_computation | async-start | bytes 2097152 | tf_op jit(solution)/shard_map/all_to_all | solution.py:28
  134.7 1.0 copy-start.3
  139.0 35.1 %all-to-all-start.2 = ((f32[8,256,256]{2,1,0:T(8,128)}), f32[8,256,256]{2,1,0:T(8,128)S(1)}, u32[]{:S(2)}, u32[]{:S(2)}) async-start(f32[8,256,256]{2,1,0:T(8,128)} %broadcast_in_dim.14), calls=%async_computation.2 | async-start | bytes 4194304 | tf_op jit(solution)/shard_map/all_to_all | solution.py:11
  174.3 60.2 %copy-start.1 = (f32[1024,256]{0,1:T(8,128)S(1)}, f32[1024,256]{0,1:T(8,128)}, u32[]{:S(2)}) copy-start(f32[1024,256]{0,1:T(8,128)} %copy.24) | copy-start | bytes 3145732
  374.5 1.0 copy-start.4
  378.8 34.6 %all-to-all-start.6 = ((f32[8,256,256]{2,1,0:T(8,128)}), f32[8,256,256]{2,1,0:T(8,128)S(1)}, u32[]{:S(2)}, u32[]{:S(2)}) async-start(f32[8,256,256]{2,1,0:T(8,128)} %broadcast_in_dim.17), calls=%async_computation.6 | async-start | bytes 4194304 | tf_op jit(solution)/shard_map/all_to_all | solution.py:11
  413.6 60.8 %copy-start.2 = (f32[1024,256]{0,1:T(8,128)S(1)}, f32[1024,256]{0,1:T(8,128)}, u32[]{:S(2)}) copy-start(f32[1024,256]{0,1:T(8,128)} %copy.27) | copy-start | bytes 3145732
  478.3 18.8 %all-to-all-start.7 = ((f32[8,256,128]{2,1,0:T(8,128)}), f32[8,256,128]{2,1,0:T(8,128)S(1)}, u32[]{:S(2)}, u32[]{:S(2)}) async-start(f32[8,256,128]{2,1,0:T(8,128)} %broadcast_in_dim.18), calls=%async_computation.7 | async-start | bytes 2097152 | tf_op jit(solution)/shard_map/all_to_all | solution.py:11
where the time goes:
time: 503 us; the launch traced here: 498 us
  blocking collectives  196 us (39%)
  other arithmetic  111 us (22%)
  waiting for transfers between devices  109 us (22%)
  starting transfers between devices  40.4 us (8%)
  local copies, waits for them, and re-layouts  23.9 us (5%)
  matrix products  14.1 us (3%)
    all_to_all x3, blocking collectives, copy_for_each(): lax.all_to_all(jnp.broadcast_to(array[None], (length, *array.shape)), axi...  139 us
    another operation x13, other arithmetic, upper_factor(): return jnp.linalg.cholesky(gram).T  68.7 us
    all_to_all x3, waiting for transfers between devices, copy_for_each(): lax.all_to_all(jnp.broadcast_to(array[None], (length, *array.shape)), axi...  58.6 us
    all_to_all x1, blocking collectives, summed_on_arrival(): lax.all_to_all(tiles, axis, split_axis=0, concat_axis=0, tiled=True)  56.7 us
    all_to_all x1, waiting for transfers between devices, summed_on_arrival(): lax.all_to_all(tiles, axis, split_axis=0, concat_axis=0, tiled=True)  50.4 us
    another operation x5, other arithmetic, apply_inverse(): solved = jax.scipy.linalg.solve_triangular(upper.T, sample.T, lower=True)  39.8 us
    all_to_all x3, starting transfers between devices, copy_for_each(): lax.all_to_all(jnp.broadcast_to(array[None], (length, *array.shape)), axi...  21.2 us
    all_to_all x1, starting transfers between devices, summed_on_arrival(): lax.all_to_all(tiles, axis, split_axis=0, concat_axis=0, tiled=True)  19.3 us
  transfers between devices with their start and end apart: 4, of which 4 were waited for; matrix products, arithmetic and copies ran while one was open for 2% of the time, Pallas kernels for 0%

commit v1 on v0

v1 whole, which is shorter than its diff:
```python
import jax
import jax.numpy as jnp
from jax import lax
from jax.sharding import Mesh, PartitionSpec as P

M = 8192
NEAR = ("y", "z_low")
FAR = "z_high"
ROWS = ("inner", "outer")


def dot(left, right, dims):
    return lax.dot_general(
        left,
        right,
        (dims, ((), ())),
        precision=lax.Precision.HIGHEST,
        preferred_element_type=jnp.float32,
    )


def scatter_sum(array, axis):
    tiles = array.reshape(lax.axis_size(axis), -1, array.shape[-1])
    return lax.all_to_all(tiles, axis, 0, 0, tiled=True).sum(axis=0)


def spread(array, axis):
    copies = jnp.broadcast_to(array[None], (lax.axis_size(axis), *array.shape))
    return lax.all_to_all(copies, axis, 0, 0, tiled=True)


def gather(array, axis):
    return spread(array, axis).reshape(-1, array.shape[-1])


def sum_over_columns(array):
    own = scatter_sum(scatter_sum(array, NEAR), FAR)
    return gather(gather(own, FAR), NEAR)


def sum_over_rows(array):
    return gather(scatter_sum(array, ROWS), ROWS)


def inverse_factor(gram):
    lower = jnp.linalg.cholesky(gram)
    identity = jnp.eye(gram.shape[0], dtype=gram.dtype)
    return jax.scipy.linalg.solve_triangular(lower, identity, lower=True)


def per_device(matrix, sketch):
    first = sum_over_columns(dot(matrix, sketch, ((1,), (0,))))
    transposed = spread(dot(matrix, first, ((0,), (0,))), ROWS).sum(axis=0)
    inverse_one = inverse_factor(sum_over_rows(dot(first, first, ((0,), (0,)))))
    product = sum_over_columns(dot(matrix, transposed, ((1,), (0,))))
    second = dot(product, inverse_one, ((1,), (1,)))
    gram = sum_over_rows(dot(second, second, ((0,), (0,))))
    coefficients = spread(dot(second, matrix, ((0,), (0,))), ROWS).sum(axis=0)
    inverse_two = inverse_factor(gram)
    basis = dot(second, inverse_two, ((1,), (1,)))
    projection = dot(inverse_two, coefficients, ((1,), (0,)))
    scale = lax.rsqrt(jnp.mean(projection * projection, axis=0, keepdims=True) + 1e-06)
    return (basis * jnp.sqrt(jnp.float32(M)), projection * scale)


def solution(mesh):
    columns, inner, outer = mesh.devices.shape
    split = Mesh(
        mesh.devices.reshape(4, columns // 8, 2, inner, outer),
        ("y", "z_high", "z_low", "inner", "outer"),
    )
    column = ("y", "z_high", "z_low")
    return jax.shard_map(
        per_device,
        mesh=split,
        in_specs=(P(ROWS, column), P(column, None)),
        out_specs=(P(ROWS, None), P(None, column)),
        check_vma=False,
    )
```

time: 503 us -> 359 us (0.71)
  blocking collectives: 196 us -> 114 us
  waiting for transfers between devices: 109 us -> 53.6 us
  local copies, waits for them, and re-layouts: 23.9 us -> 16.9 us
    all_to_all x4 -> x6, blocking collectives: 196 us -> 114 us  [the longest x4 71.3 us: spread(): return lax.all_to_all(copies, axis, 0, 0, tiled=True)]
    all_to_all x4 -> x8, waiting for transfers between devices: 109 us -> 53.6 us  [the longest x4 42.3 us: scatter_sum(): return lax.all_to_all(tiles, axis, 0, 0, tiled=True).sum(axis=0)]
    dot_general x6 -> x9, matrix products: 9.5 us -> 15.7 us  [dot(): lax.dot_general(left, right, (dims, ((), ())), precision=lax.Precision.HI...]
    all_to_all x4 -> x8, starting transfers between devices: 40.4 us -> 35.7 us  [the longest x4 17.9 us: spread(): return lax.all_to_all(copies, axis, 0, 0, tiled=True)]
  transfers between devices with their start and end apart: 4 -> 8, of which waited for: 4 -> 6; matrix products, arithmetic and copies ran while one was open for 2% -> 36% of each run, Pallas kernels for 0% -> 0%
where the time goes in v1:
time: 359 us; the launch traced here: 352 us
  blocking collectives  114 us (32%)
  other arithmetic  110 us (31%)
  waiting for transfers between devices  53.6 us (15%)
  starting transfers between devices  35.7 us (10%)
  matrix products  18.4 us (5%)
  local copies, waits for them, and re-layouts  16.9 us (5%)
  between operations  4.06 us (1%)
    all_to_all x4, blocking collectives, spread(): return lax.all_to_all(copies, axis, 0, 0, tiled=True)  71.3 us
    another operation x13, other arithmetic, inverse_factor(): lower = jnp.linalg.cholesky(gram)  68.6 us
    all_to_all x2, blocking collectives, scatter_sum(): return lax.all_to_all(tiles, axis, 0, 0, tiled=True).sum(axis=0)  42.6 us
    all_to_all x4, waiting for transfers between devices, scatter_sum(): return lax.all_to_all(tiles, axis, 0, 0, tiled=True).sum(axis=0)  42.3 us
    another operation x5, other arithmetic, inverse_factor(): return jax.scipy.linalg.solve_triangular(lower, identity, lower=True)  39.9 us
    all_to_all x4, starting transfers between devices, spread(): return lax.all_to_all(copies, axis, 0, 0, tiled=True)  17.9 us
    all_to_all x4, starting transfers between devices, scatter_sum(): return lax.all_to_all(tiles, axis, 0, 0, tiled=True).sum(axis=0)  17.8 us
    dot_general x9, matrix products, dot(): lax.dot_general(left, right, (dims, ((), ())), precision=lax.Precision.HI...  15.7 us
  transfers between devices with their start and end apart: 8, of which 6 were waited for; matrix products, arithmetic and copies ran while one was open for 36% of the time, Pallas kernels for 0%

profile of v1, /device:TPU:1, one launch (start us, length us, event | category | flops | bytes accessed | tf_op | source)
XLA Modules:
  0.0 352.3 jit_solution(12678067093156789815)
XLA Ops:
  1.7 2.8 fusion.27
  4.5 6.4 %all-to-all-start = ((f32[8,128,256]{2,1,0:T(8,128)}), f32[8,128,256]{2,1,0:T(8,128)S(1)}, u32[]{:S(2)}, u32[]{:S(2)}) async-start(f32[8,128,256]{2,1,0:T(8,128)} %bitcast), calls=%async_computation | async-start | bytes 2097152 | tf_op jit(solution)/shard_map/all_to_all | solution.py:24
  10.9 11.9 %all-to-all-done = f32[8,128,256]{2,1,0:T(8,128)S(1)} async-done(((f32[8,128,256]{2,1,0:T(8,128)}), f32[8,128,256]{2,1,0:T(8,128)S(1)}, u32[]{:S(2)}, u32[]{:S(2)}) %all-to-all-start) | async-done | bytes 1048608 | tf_op jit(solution)/shard_map/all_to_all | solution.py:24
  22.9 30.1 %all_to_all.73 = f32[8,16,256]{2,1,0:T(8,128)S(1)} all-to-all(f32[8,16,256]{2,1,0:T(8,128)S(1)} %bitcast.111), channel_id=1, replica_groups=mesh['y'=4,'z_high'=8,'z_low'=2,'inner'=2,'outer'=4] {'z_high'}, dimensions={0} | all-to-all | bytes 262144 | tf_op jit(solution)/shard_map/all_to_all | solution.py:24
  53.0 15.5 %all_to_all.70 = f32[8,16,256]{2,1,0:T(8,128)S(1)} all-to-all(f32[8,16,256]{2,1,0:T(8,128)S(1)} %broadcast_in_dim.21), channel_id=1, replica_groups=mesh['y'=4,'z_high'=8,'z_low'=2,'inner'=2,'outer'=4] {'z_high'}, dimensions={0} | all-to-all | bytes 262144 | tf_op jit(solution)/shard_map/all_to_all | solution.py:29
  68.6 16.8 %all_to_all.71 = f32[8,128,256]{2,1,0:T(8,128)S(1)} all-to-all(f32[8,128,256]{2,1,0:T(8,128)S(1)} %broadcast_in_dim.23), channel_id=1, replica_groups=mesh['y'=4,'z_high'=8,'z_low'=2,'inner'=2,'outer'=4] {'y','z_low'}, dimensions={0} | all-to-all | bytes 2097152 | tf_op jit(solution)/shard_map/all_to_all | solution.py:29
  87.4 23.3 %all_to_all.74 = f32[8,128,256]{2,1,0:T(8,128)S(1)} all-to-all(f32[8,128,256]{2,1,0:T(8,128)S(1)} %broadcast_in_dim.24), channel_id=1, replica_groups=mesh['y'=4,'z_high'=8,'z_low'=2,'inner'=2,'outer'=4] {'inner','outer'}, dimensions={0} | all-to-all | bytes 2097152 | tf_op jit(solution)/shard_map/all_to_all | solution.py:29
  112.8 3.6 %all-to-all-start.5 = ((f32[8,128,256]{1,2,0:T(8,128)}), f32[8,128,256]{1,2,0:T(8,128)S(1)}, u32[]{:S(2)}, u32[]{:S(2)}) async-start(f32[8,128,256]{1,2,0:T(8,128)} %bitcast.106), calls=%async_computation.5 | async-start | bytes 2097152 | tf_op jit(solution)/shard_map/all_to_all | solution.py:24
  117.7 3.0 fusion.28
  120.7 11.1 %all-to-all-done.5 = f32[8,128,256]{1,2,0:T(8,128)S(1)} async-done(((f32[8,128,256]{1,2,0:T(8,128)}), f32[8,128,256]{1,2,0:T(8,128)S(1)}, u32[]{:S(2)}, u32[]{:S(2)}) %all-to-all-start.5) | async-done | bytes 1048608 | tf_op jit(solution)/shard_map/all_to_all | solution.py:24
  131.8 4.5 %all-to-all-start.9 = ((f32[8,32,256]{2,1,0:T(8,128)}), f32[8,32,256]{2,1,0:T(8,128)S(1)}, u32[]{:S(2)}, u32[]{:S(2)}) async-start(f32[8,32,256]{2,1,0:T(8,128)} %fusion.28), calls=%async_computation.9 | async-start | bytes 524288 | tf_op jit(solution)/shard_map/all_to_all | solution.py:24
  137.2 5.7 %all-to-all-done.9 = f32[8,32,256]{2,1,0:T(8,128)S(1)} async-done(((f32[8,32,256]{2,1,0:T(8,128)}), f32[8,32,256]{2,1,0:T(8,128)S(1)}, u32[]{:S(2)}, u32[]{:S(2)}) %all-to-all-start.9) | async-done | bytes 262176 | tf_op jit(solution)/shard_map/all_to_all | solution.py:24
  142.9 3.4 all-to-all-start.6
  146.3 13.5 %all-to-all-done.6 = f32[8,16,256]{2,1,0:T(8,128)S(1)} async-done(((f32[8,16,256]{2,1,0:T(8,128)}), f32[8,16,256]{2,1,0:T(8,128)S(1)}, u32[]{:S(2)}, u32[]{:S(2)}) %all-to-all-start.6) | async-done | bytes 131104 | tf_op jit(solution)/shard_map/all_to_all | solution.py:24
  160.6 6.4 %all-to-all-start.10 = ((f32[8,32,256]{2,1,0:T(8,128)}), f32[8,32,256]{2,1,0:T(8,128)S(1)}, u32[]{:S(2)}, u32[]{:S(2)}) async-start(f32[8,32,256]{2,1,0:T(8,128)} %broadcast_in_dim.28), calls=%async_computation.10 | async-start | bytes 524288 | tf_op jit(solution)/shard_map/all_to_all | solution.py:29
  167.0 6.5 %all-to-all-done.10 = f32[8,32,256]{2,1,0:T(8,128)S(1)} async-done(((f32[8,32,256]{2,1,0:T(8,128)}), f32[8,32,256]{2,1,0:T(8,128)S(1)}, u32[]{:S(2)}, u32[]{:S(2)}) %all-to-all-start.10) | async-done | bytes 262176 | tf_op jit(solution)/shard_map/all_to_all | solution.py:29
  173.5 15.6 %all_to_all.72 = f32[8,16,256]{2,1,0:T(8,128)S(1)} all-to-all(f32[8,16,256]{2,1,0:T(8,128)S(1)} %broadcast_in_dim.25), channel_id=1, replica_groups=mesh['y'=4,'z_high'=8,'z_low'=2,'inner'=2,'outer'=4] {'z_high'}, dimensions={0} | all-to-all | bytes 262144 | tf_op jit(solution)/shard_map/all_to_all | solution.py:29
  190.2 3.7 %all-to-all-start.8 = ((f32[8,128,256]{2,1,0:T(8,128)}), f32[8,128,256]{2,1,0:T(8,128)S(1)}, u32[]{:S(2)}, u32[]{:S(2)}) async-start(f32[8,128,256]{2,1,0:T(8,128)} %broadcast_in_dim.27), calls=%async_computation.8 | async-start | bytes 2097152 | tf_op jit(solution)/shard_map/all_to_all | solution.py:29
  194.2 11.7 %cholesky.130 = f32[128,128]{1,0:T(8,128)S(1)} custom-call(f32[128,128]{1,0:T(8,128)S(1)} %cholesky.194), custom_call_target="Cholesky" | custom-call | tf_op jit(solution)/shard_map/jit(cholesky)/cholesky | solution.py:46
  206.0 9.8 %custom-call.13 = f32[1,128,128]{1,2,0:T(8,128)S(1)} custom-call(f32[1,128,128]{2,1,0:T(8,128)S(1)} %get-tuple-element.47), custom_call_target="InvertDiagBlocksLowerTriangular" | custom-call | tf_op jit(solution)/shard_map/jit(cholesky)/cholesky | solution.py:46
  216.3 11.7 %cholesky.147 = f32[128,128]{1,0:T(8,128)S(1)} custom-call(f32[128,128]{1,0:T(8,128)S(1)} %convolution_subtract_fusion.3), custom_call_target="Cholesky" | custom-call | tf_op jit(solution)/shard_map/jit(cholesky)/cholesky | solution.py:46
  230.0 3.8 %while.4 = (s32[]{:T(128)}, f32[256,256]{1,0:T(8,128)S(1)}, s32[2,2]{1,0:T(2,128)S(1)}, f32[2,128,128]{2,1,0:T(8,128)S(1)}, s32[]{:T(128)}) while((s32[]{:T(128)}, f32[256,256]{1,0:T(8,128)S(1)}, s32[2,2]{1,0:T(2,128)S(1)}, f32[2,128,128]{2,1,0:T(8,128)S(1)}, s32[]{:T(128)}) %tuple.48), condition=%wide.while_cond, body=%wide.while_body.sunk | while | flops 2 | bytes 131181 | solution.py:48
  233.8 19.9 %custom-call.14 = f32[2,128,128]{1,2,0:T(8,128)S(1)} custom-call(f32[2,128,128]{2,1,0:T(8,128)S(1)} %get-tuple-element.18), custom_call_target="InvertDiagBlocksLowerTriangular" | custom-call | tf_op jit(solution)/shard_map/jit(_solve_triangular)/triangular_solve | solution.py:48
  257.5 12.5 %all_to_all.75 = f32[8,32,256]{2,1,0:T(8,128)S(1)} all-to-all(f32[8,32,256]{2,1,0:T(8,128)S(1)} %bitcast.110), channel_id=1, replica_groups=mesh['y'=4,'z_high'=8,'z_low'=2,'inner'=2,'outer'=4] {'inner','outer'}, dimensions={0} | all-to-all | bytes 524288 | tf_op jit(solution)/shard_map/all_to_all | solution.py:24
  270.8 3.7 %all-to-all-start.12 = ((f32[8,32,256]{2,1,0:T(8,128)}), f32[8,32,256]{2,1,0:T(8,128)S(1)}, u32[]{:S(2)}, u32[]{:S(2)}) async-start(f32[8,32,256]{2,1,0:T(8,128)} %broadcast_in_dim.29), calls=%async_computation.12 | async-start | bytes 524288 | tf_op jit(solution)/shard_map/all_to_all | solution.py:29
  276.2 4.7 %all-to-all-done.12 = f32[8,32,256]{2,1,0:T(8,128)S(1)} async-done(((f32[8,32,256]{2,1,0:T(8,128)}), f32[8,32,256]{2,1,0:T(8,128)S(1)}, u32[]{:S(2)}, u32[]{:S(2)}) %all-to-all-start.12) | async-done | bytes 262176 | tf_op jit(solution)/shard_map/all_to_all | solution.py:29
  282.0 4.1 %all-to-all-start.13 = ((f32[8,256,128]{2,1,0:T(8,128)}), f32[8,256,128]{2,1,0:T(8,128)S(1)}, u32[]{:S(2)}, u32[]{:S(2)}) async-start(f32[8,256,128]{2,1,0:T(8,128)} %broadcast_in_dim.30), calls=%async_computation.13 | async-start | bytes 2097152 | tf_op jit(solution)/shard_map/all_to_all | solution.py:29
  287.0 11.7 %cholesky.164 = f32[128,128]{1,0:T(8,128)S(1)} custom-call(f32[128,128]{1,0:T(8,128)S(1)} %cholesky.197), custom_call_target="Cholesky" | custom-call | tf_op jit(solution)/shard_map/jit(cholesky)/cholesky | solution.py:46
  298.8 9.8 %custom-call.15 = f32[1,128,128]{1,2,0:T(8,128)S(1)} custom-call(f32[1,128,128]{2,1,0:T(8,128)S(1)} %get-tuple-element.43), custom_call_target="InvertDiagBlocksLowerTriangular" | custom-call | tf_op jit(solution)/shard_map/jit(cholesky)/cholesky | solution.py:46
  309.1 11.7 %cholesky.181 = f32[128,128]{1,0:T(8,128)S(1)} custom-call(f32[128,128]{1,0:T(8,128)S(1)} %convolution_subtract_fusion.2), custom_call_target="Cholesky" | custom-call | tf_op jit(solution)/shard_map/jit(cholesky)/cholesky | solution.py:46
  323.6 4.1 %while.5 = (s32[]{:T(128)}, f32[256,256]{1,0:T(8,128)S(1)}, s32[2,2]{1,0:T(2,128)S(1)}, f32[2,128,128]{2,1,0:T(8,128)S(1)}, s32[]{:T(128)}) while((s32[]{:T(128)}, f32[256,256]{1,0:T(8,128)S(1)}, s32[2,2]{1,0:T(2,128)S(1)}, f32[2,128,128]{2,1,0:T(8,128)S(1)}, s32[]{:T(128)}) %tuple.54), condition=%wide.while_cond.clone, body=%wide.while_body.clone.sunk | while | flops 2 | bytes 131181 | solution.py:48
  327.7 20.0 %custom-call.16 = f32[2,128,128]{1,2,0:T(8,128)S(1)} custom-call(f32[2,128,128]{2,1,0:T(8,128)S(1)} %get-tuple-element.19), custom_call_target="InvertDiagBlocksLowerTriangular" | custom-call | tf_op jit(solution)/shard_map/jit(_solve_triangular)/triangular_solve | solution.py:48
  (81 shorter events, 32.8 us)
Async XLA Ops:
  0.6 1.0 copy-start
  4.5 18.3 %all-to-all-start = ((f32[8,128,256]{2,1,0:T(8,128)}), f32[8,128,256]{2,1,0:T(8,128)S(1)}, u32[]{:S(2)}, u32[]{:S(2)}) async-start(f32[8,128,256]{2,1,0:T(8,128)} %bitcast), calls=%async_computation | async-start | bytes 2097152 | tf_op jit(solution)/shard_map/all_to_all | solution.py:24
  112.8 19.0 %all-to-all-start.5 = ((f32[8,128,256]{1,2,0:T(8,128)}), f32[8,128,256]{1,2,0:T(8,128)S(1)}, u32[]{:S(2)}, u32[]{:S(2)}) async-start(f32[8,128,256]{1,2,0:T(8,128)} %bitcast.106), calls=%async_computation.5 | async-start | bytes 2097152 | tf_op jit(solution)/shard_map/all_to_all | solution.py:24
  131.8 11.1 %all-to-all-start.9 = ((f32[8,32,256]{2,1,0:T(8,128)}), f32[8,32,256]{2,1,0:T(8,128)S(1)}, u32[]{:S(2)}, u32[]{:S(2)}) async-start(f32[8,32,256]{2,1,0:T(8,128)} %fusion.28), calls=%async_computation.9 | async-start | bytes 524288 | tf_op jit(solution)/shard_map/all_to_all | solution.py:24
  142.9 16.9 %all-to-all-start.6 = ((f32[8,16,256]{2,1,0:T(8,128)}), f32[8,16,256]{2,1,0:T(8,128)S(1)}, u32[]{:S(2)}, u32[]{:S(2)}) async-start(f32[8,16,256]{2,1,0:T(8,128)} %bitcast.6), calls=%async_computation.6 | async-start | bytes 262144 | tf_op jit(solution)/shard_map/all_to_all | solution.py:24
  160.6 13.0 %all-to-all-start.10 = ((f32[8,32,256]{2,1,0:T(8,128)}), f32[8,32,256]{2,1,0:T(8,128)S(1)}, u32[]{:S(2)}, u32[]{:S(2)}) async-start(f32[8,32,256]{2,1,0:T(8,128)} %broadcast_in_dim.28), calls=%async_computation.10 | async-start | bytes 524288 | tf_op jit(solution)/shard_map/all_to_all | solution.py:29
  190.2 64.4 %all-to-all-start.8 = ((f32[8,128,256]{2,1,0:T(8,128)}), f32[8,128,256]{2,1,0:T(8,128)S(1)}, u32[]{:S(2)}, u32[]{:S(2)}) async-start(f32[8,128,256]{2,1,0:T(8,128)} %broadcast_in_dim.27), calls=%async_computation.8 | async-start | bytes 2097152 | tf_op jit(solution)/shard_map/all_to_all | solution.py:29
  270.8 10.2 %all-to-all-start.12 = ((f32[8,32,256]{2,1,0:T(8,128)}), f32[8,32,256]{2,1,0:T(8,128)S(1)}, u32[]{:S(2)}, u32[]{:S(2)}) async-start(f32[8,32,256]{2,1,0:T(8,128)} %broadcast_in_dim.29), calls=%async_computation.12 | async-start | bytes 524288 | tf_op jit(solution)/shard_map/all_to_all | solution.py:29
  282.0 68.6 %all-to-all-start.13 = ((f32[8,256,128]{2,1,0:T(8,128)}), f32[8,256,128]{2,1,0:T(8,128)S(1)}, u32[]{:S(2)}, u32[]{:S(2)}) async-start(f32[8,256,128]{2,1,0:T(8,128)} %broadcast_in_dim.30), calls=%async_computation.13 | async-start | bytes 2097152 | tf_op jit(solution)/shard_map/all_to_all | solution.py:29
  286.3 0.7 copy-start.1
  287.0 21.6 %copy-start.2 = (f32[256,256]{1,0:T(8,128)S(1)}, f32[256,256]{1,0:T(8,128)}, u32[]{:S(2)}) copy-start(f32[256,256]{1,0:T(8,128)} %copy-done.1) | copy-start | bytes 786436

commit v2 on v1

v2 whole, which is shorter than its diff:
```python
import functools

import jax
import jax.numpy as jnp
from jax import lax
from jax.experimental import pallas as pl
from jax.experimental.pallas import tpu as pltpu
from jax.sharding import Mesh, PartitionSpec as P

M = 8192
NEAR = ("y", "z_low")
FAR = "z_high"
ROWS = ("inner", "outer")
STEP = 8
LANES = 128
BLOCK = 64


def dot(left, right, dims):
    return lax.dot_general(
        left,
        right,
        (dims, ((), ())),
        precision=lax.Precision.HIGHEST,
        preferred_element_type=jnp.float32,
    )


def factor_rows(tiles, first):
    depth = len(tiles)
    row = lax.broadcasted_iota(jnp.int32, (STEP, LANES), 0)
    roots = []
    for panel in range(depth):
        columns = []
        for i in range(STEP):
            tile, lane = divmod(first + panel * STEP + i, LANES)
            columns.append(
                [
                    jnp.broadcast_to(tiles[s][tile][:, lane : lane + 1], (STEP, LANES))
                    for s in range(panel, depth)
                ]
            )
        scale = jnp.zeros((STEP, LANES), jnp.float32)
        for i in range(STEP):
            root = lax.rsqrt(columns[i][0][i : i + 1, :])
            inverse = root * root
            scale = jnp.where(row == i, root, scale)
            weights = [column * inverse for column in columns[i]]
            weights[0] = jnp.where(row > i, weights[0], 0.0)
            for j in range(i + 1, STEP):
                partner = columns[i][0][j : j + 1, :]
                columns[j] = [c - w * partner for c, w in zip(columns[j], weights)]
            for t in range(len(tiles[panel])):
                source = tiles[panel][t][i : i + 1, :]
                for s in range(panel, depth):
                    tiles[s][t] = tiles[s][t] - weights[s - panel] * source
        roots.append(scale)
    return [[tile * roots[s] for tile in tiles[s]] for s in range(depth)]


def inverse_kernel(gram_ref, out_ref, work_ref):
    size = gram_ref.shape[0]
    rows = lax.broadcasted_iota(jnp.int32, (size, size), 0)
    lanes = lax.broadcasted_iota(jnp.int32, (size, size), 1)
    work_ref[:, :size] = gram_ref[...]
    work_ref[:, size:] = jnp.where(rows == lanes, 1.0, 0.0).astype(jnp.float32)
    for start in range(0, size, BLOCK):
        rest = start + BLOCK
        low = start // LANES * LANES
        high = size + -(-rest // LANES) * LANES
        tiles = [
            [
                work_ref[pl.ds(start + s, STEP), pl.ds(t, LANES)]
                for t in range(low, high, LANES)
            ]
            for s in range(0, BLOCK, STEP)
        ]
        tiles = factor_rows(tiles, start - low)
        whole = jnp.concatenate([jnp.concatenate(r, axis=1) for r in tiles], axis=0)
        out_ref[pl.ds(start, BLOCK), : high - size] = whole[:, size - low :]
        if high < 2 * size:
            out_ref[pl.ds(start, BLOCK), high - size :] = jnp.zeros(
                (BLOCK, 2 * size - high), jnp.float32
            )
        if rest < size:
            base = rest // LANES * LANES
            left = whole[:, base - low : size - low].T[rest - base :, :]
            work_ref[pl.ds(rest, size - rest), pl.ds(low, high - low)] -= dot(
                left, whole, ((1,), (0,))
            )


def inverse_factor(gram):
    size = gram.shape[0]
    return pl.pallas_call(
        inverse_kernel,
        out_shape=jax.ShapeDtypeStruct(gram.shape, jnp.float32),
        in_specs=[pl.BlockSpec(memory_space=pltpu.VMEM)],
        out_specs=pl.BlockSpec(memory_space=pltpu.VMEM),
        scratch_shapes=[pltpu.VMEM((size, 2 * size), jnp.float32)],
        cost_estimate=pl.CostEstimate(
            flops=2_000_000_000, transcendentals=size, bytes_accessed=8 * size * size
        ),
        name="inverse_factor",
    )(gram)


def exchange(tiles, axis):
    return lax.all_to_all(tiles, axis, 0, 0, tiled=True)


def tiles_for(array, axis):
    return array.reshape(lax.axis_size(axis), -1, array.shape[-1])


def copies_for(array, axis):
    return jnp.broadcast_to(array[None], (lax.axis_size(axis), *array.shape))


def scatter_sum(array, axis):
    return exchange(tiles_for(array, axis), axis).sum(axis=0)


def gather(array, axis):
    return exchange(copies_for(array, axis), axis).reshape(-1, array.shape[-1])


def sum_over_rows(array):
    return gather(scatter_sum(array, ROWS), ROWS)


def per_device(matrix, sketch):
    near = lax.axis_size(NEAR)
    rank = sketch.shape[1]
    width = matrix.shape[1]
    part = rank // near

    partial = dot(matrix, sketch, ((1,), (0,)))
    own = scatter_sum(scatter_sum(partial, NEAR), FAR)
    first = gather(gather(own, FAR), NEAR)

    own_gram = lax.dynamic_slice_in_dim(
        dot(first, first, ((0,), (0,))), lax.axis_index(NEAR) * part, part, 0
    )
    summed = sum_over_rows(
        jnp.concatenate([dot(matrix, first, ((0,), (0,))), own_gram], axis=0)
    )
    transposed, own_gram = summed[:width], summed[width:]

    partial = tiles_for(dot(matrix, transposed, ((1,), (0,))), NEAR)
    arrived = exchange(jnp.concatenate([partial, copies_for(own_gram, NEAR)], axis=1), NEAR)
    gram = arrived[:, -part:].reshape(rank, rank)
    own = scatter_sum(arrived[:, :-part].sum(axis=0), FAR)
    own = dot(own, inverse_factor(gram), ((1,), (1,)))
    second = gather(gather(own, FAR), NEAR)

    summed = sum_over_rows(
        jnp.concatenate(
            [dot(second, second, ((0,), (0,))), dot(matrix, second, ((0,), (0,)))], axis=0
        )
    )
    inverse = inverse_factor(summed[:rank])
    basis = dot(second, inverse, ((1,), (1,)))
    projection = dot(inverse, summed[rank:], ((1,), (1,)))
    scale = lax.rsqrt(jnp.mean(projection * projection, axis=0, keepdims=True) + 1e-06)
    return (basis * jnp.sqrt(jnp.float32(M)), projection * scale)


def solution(mesh):
    columns, inner, outer = mesh.devices.shape
    split = Mesh(
        mesh.devices.reshape(4, columns // 8, 2, inner, outer),
        ("y", "z_high", "z_low", "inner", "outer"),
    )
    column = ("y", "z_high", "z_low")
    return jax.shard_map(
        per_device,
        mesh=split,
        in_specs=(P(ROWS, column), P(column, None)),
        out_specs=(P(ROWS, None), P(None, column)),
        check_vma=False,
    )
```

time: 359 us -> 234 us (0.65); the launches traced: 352 us -> 233 us
  other arithmetic: 110 us -> 1.66 us
  blocking collectives: 114 us -> 171 us
  waiting for transfers between devices: 53.6 us -> 14.3 us
  starting transfers between devices: 35.7 us -> 7.11 us
  Pallas kernels: 0 us -> 19.5 us
  local copies, waits for them, and re-layouts: 16.9 us -> 4.15 us
  matrix products: 18.4 us -> 14.1 us
    another operation x18 -> x0, other arithmetic: 109 us -> none  [the longest x13 68.6 us: inverse_factor(): lower = jnp.linalg.cholesky(gram)]
    all_to_all x6 -> x10, blocking collectives: 114 us -> 171 us  [exchange(): return lax.all_to_all(tiles, axis, 0, 0, tiled=True)]
    all_to_all x8 -> x2, waiting for transfers between devices: 53.6 us -> 14.3 us  [exchange(): return lax.all_to_all(tiles, axis, 0, 0, tiled=True)]
    all_to_all x8 -> x2, starting transfers between devices: 35.7 us -> 7.11 us  [exchange(): return lax.all_to_all(tiles, axis, 0, 0, tiled=True)]
    pallas_call x0 -> x2, Pallas kernels: none -> 19.5 us  [inverse_factor(): pl.pallas_call(inverse_kernel, out_shape=jax.ShapeDtypeStruct(gram.shape,...]
    another operation x19 -> x0, local copies, waits for them, and re-layouts: 7.93 us -> none  [the longest x15 7.88 us: inverse_factor(): return jax.scipy.linalg.solve_triangular(lower, identity, lower=True)]
  transfers between devices with their start and end apart: 8 -> 2, of which waited for: 6 -> 2; matrix products, arithmetic and copies ran while one was open for 36% -> 0% of each run, Pallas kernels for 0% -> 4%
where the time goes in v2:
time: 234 us; the launch traced here: 233 us
  blocking collectives  171 us (73%)
  Pallas kernels  19.5 us (8%)
  waiting for transfers between devices  14.3 us (6%)
  matrix products  14.1 us (6%)
  starting transfers between devices  7.11 us (3%)
  local copies, waits for them, and re-layouts  4.15 us (2%)
    all_to_all x10, blocking collectives, exchange(): return lax.all_to_all(tiles, axis, 0, 0, tiled=True)  171 us
    pallas_call x2, Pallas kernels, inverse_factor(): pl.pallas_call(inverse_kernel, out_shape=jax.ShapeDtypeStruct(gram.shape,...  19.5 us
    all_to_all x2, waiting for transfers between devices, exchange(): return lax.all_to_all(tiles, axis, 0, 0, tiled=True)  14.3 us
    dot_general x9, matrix products, dot(): lax.dot_general(left, right, (dims, ((), ())), precision=lax.Precision.HI...  14.1 us
    all_to_all x2, starting transfers between devices, exchange(): return lax.all_to_all(tiles, axis, 0, 0, tiled=True)  7.11 us
  transfers between devices with their start and end apart: 2, of which 2 were waited for; matrix products, arithmetic and copies ran while one was open for 0% of the time, Pallas kernels for 4%

profile of v2, /device:TPU:1, one launch (start us, length us, event | category | flops | bytes accessed | tf_op | source)
XLA Modules:
  0.0 232.7 jit_solution(721136290278081356)
XLA Ops:
  0.6 1.0 copy-done
  1.7 1.9 fusion.3
  3.6 18.9 %all_to_all.60 = f32[8,128,256]{2,1,0:T(8,128)S(1)} all-to-all(f32[8,128,256]{2,1,0:T(8,128)S(1)} %bitcast.41), channel_id=1, replica_groups=mesh['y'=4,'z_high'=8,'z_low'=2,'inner'=2,'outer'=4] {'y','z_low'}, dimensions={0} | all-to-all | bytes 2097152 | tf_op jit(solution)/shard_map/all_to_all | solution.py:109
  22.5 28.9 %all_to_all.61 = f32[8,16,256]{2,1,0:T(8,128)S(1)} all-to-all(f32[8,16,256]{2,1,0:T(8,128)S(1)} %bitcast.45), channel_id=1, replica_groups=mesh['y'=4,'z_high'=8,'z_low'=2,'inner'=2,'outer'=4] {'z_high'}, dimensions={0} | all-to-all | bytes 262144 | tf_op jit(solution)/shard_map/all_to_all | solution.py:109
  51.5 16.5 %all_to_all.62 = f32[8,16,256]{2,1,0:T(8,128)S(1)} all-to-all(f32[8,16,256]{2,1,0:T(8,128)S(1)} %broadcast_in_dim.18), channel_id=1, replica_groups=mesh['y'=4,'z_high'=8,'z_low'=2,'inner'=2,'outer'=4] {'z_high'}, dimensions={0} | all-to-all | bytes 262144 | tf_op jit(solution)/shard_map/all_to_all | solution.py:109
  67.9 1.1 broadcast_in_dim.20
  69.0 3.6 %all-to-all-start.3 = ((f32[8,128,256]{2,1,0:T(8,128)}), f32[8,128,256]{2,1,0:T(8,128)S(1)}, u32[]{:S(2)}, u32[]{:S(2)}) async-start(f32[8,128,256]{2,1,0:T(8,128)} %broadcast_in_dim.20), calls=%async_computation.3 | async-start | bytes 2097152 | tf_op jit(solution)/shard_map/all_to_all | solution.py:109
  72.6 11.8 %all-to-all-done.3 = f32[8,128,256]{2,1,0:T(8,128)S(1)} async-done(((f32[8,128,256]{2,1,0:T(8,128)}), f32[8,128,256]{2,1,0:T(8,128)S(1)}, u32[]{:S(2)}, u32[]{:S(2)}) %all-to-all-start.3) | async-done | bytes 1048608 | tf_op jit(solution)/shard_map/all_to_all | solution.py:109
  84.4 1.0 convolution_bitcast_fusion.4
  85.4 1.8 convolution_bitcast_fusion.2
  87.3 14.8 %all_to_all.63 = f32[8,20,256]{2,1,0:T(8,128)S(1)} all-to-all(f32[8,20,256]{2,1,0:T(8,128)S(1)} %reshape.55), channel_id=1, replica_groups=mesh['y'=4,'z_high'=8,'z_low'=2,'inner'=2,'outer'=4] {'inner','outer'}, dimensions={0} | all-to-all | bytes 327680 | tf_op jit(solution)/shard_map/all_to_all | solution.py:109
  102.2 9.0 %all_to_all.64 = f32[8,20,256]{2,1,0:T(8,128)S(1)} all-to-all(f32[8,20,256]{2,1,0:T(8,128)S(1)} %broadcast_in_dim.21), channel_id=1, replica_groups=mesh['y'=4,'z_high'=8,'z_low'=2,'inner'=2,'outer'=4] {'inner','outer'}, dimensions={0} | all-to-all | bytes 327680 | tf_op jit(solution)/shard_map/all_to_all | solution.py:109
  111.2 1.0 convolution_bitcast_fusion
  112.3 0.3 copy.15
  112.7 20.3 %all_to_all.65 = f32[8,160,256]{2,1,0:T(8,128)S(1)} all-to-all(f32[8,160,256]{2,1,0:T(8,128)S(1)} %pad_maximum_fusion), channel_id=1, replica_groups=mesh['y'=4,'z_high'=8,'z_low'=2,'inner'=2,'outer'=4] {'y','z_low'}, dimensions={0} | all-to-all | bytes 2621440 | tf_op jit(solution)/shard_map/all_to_all | solution.py:109
  133.0 0.7 slice_reduce_fusion
  133.7 3.6 %all-to-all-start.7 = ((f32[8,16,256]{2,1,0:T(8,128)}), f32[8,16,256]{2,1,0:T(8,128)S(1)}, u32[]{:S(2)}, u32[]{:S(2)}) async-start(f32[8,16,256]{2,1,0:T(8,128)} %bitcast.8), calls=%async_computation.7 | async-start | bytes 262144 | tf_op jit(solution)/shard_map/all_to_all | solution.py:109
  137.3 0.7 slice.27
  138.0 9.8 %inverse_factor.2 = f32[256,256]{1,0:T(8,128)} custom-call(f32[256,256]{1,0:T(8,128)} %bitcast.48), custom_call_target="tpu_custom_call" | custom-call | flops 2000000000 | bytes 524288 | tf_op jit(solution)/shard_map/inverse_factor/pallas_call | solution.py:95
  147.8 2.5 %all-to-all-done.7 = f32[8,16,256]{2,1,0:T(8,128)S(1)} async-done(((f32[8,16,256]{2,1,0:T(8,128)}), f32[8,16,256]{2,1,0:T(8,128)S(1)}, u32[]{:S(2)}, u32[]{:S(2)}) %all-to-all-start.7) | async-done | bytes 131104 | tf_op jit(solution)/shard_map/all_to_all | solution.py:109
  150.3 1.2 fusion.4
  151.6 21.7 %all_to_all.66 = f32[8,16,256]{2,1,0:T(8,128)S(1)} all-to-all(f32[8,16,256]{2,1,0:T(8,128)S(1)} %broadcast_in_dim.23), channel_id=1, replica_groups=mesh['y'=4,'z_high'=8,'z_low'=2,'inner'=2,'outer'=4] {'z_high'}, dimensions={0} | all-to-all | bytes 262144 | tf_op jit(solution)/shard_map/all_to_all | solution.py:109
  173.4 14.6 %all_to_all.67 = f32[8,128,256]{2,1,0:T(8,128)S(1)} all-to-all(f32[8,128,256]{2,1,0:T(8,128)S(1)} %broadcast_in_dim.25), channel_id=1, replica_groups=mesh['y'=4,'z_high'=8,'z_low'=2,'inner'=2,'outer'=4] {'y','z_low'}, dimensions={0} | all-to-all | bytes 2097152 | tf_op jit(solution)/shard_map/all_to_all | solution.py:109
  188.0 1.0 convolution_bitcast_fusion.3
  189.1 1.8 convolution_bitcast_fusion.1
  190.9 15.1 %all_to_all.68 = f32[8,48,256]{2,1,0:T(8,128)S(1)} all-to-all(f32[8,48,256]{2,1,0:T(8,128)S(1)} %bitcast.44), channel_id=1, replica_groups=mesh['y'=4,'z_high'=8,'z_low'=2,'inner'=2,'outer'=4] {'inner','outer'}, dimensions={0} | all-to-all | bytes 786432 | tf_op jit(solution)/shard_map/all_to_all | solution.py:109
  206.1 11.2 %all_to_all.69 = f32[8,48,256]{2,1,0:T(8,128)S(1)} all-to-all(f32[8,48,256]{2,1,0:T(8,128)S(1)} %broadcast_in_dim.26), channel_id=1, replica_groups=mesh['y'=4,'z_high'=8,'z_low'=2,'inner'=2,'outer'=4] {'inner','outer'}, dimensions={0} | all-to-all | bytes 786432 | tf_op jit(solution)/shard_map/all_to_all | solution.py:109
  217.2 0.7 slice.28.gram_ref
  218.0 9.8 %inverse_factor.3 = f32[256,256]{1,0:T(8,128)} custom-call(f32[256,256]{1,0:T(8,128)} %slice.28.gram_ref), custom_call_target="tpu_custom_call" | custom-call | flops 2000000000 | bytes 524288 | tf_op jit(solution)/shard_map/inverse_factor/pallas_call | solution.py:95
  227.7 1.3 multiply_reduce_fusion
  229.1 2.9 %convolution_multiply_fusion = f32[1024,256]{1,0:T(8,128)} fusion(f32[1024,256]{1,0:T(8,128)S(1)} %bitcast.38, f32[256,256]{1,0:T(8,128)} %inverse_factor.3), kind=kOutput, calls=%fused_computation.1 | convolution fusion | flops 805568512 | bytes 2359296 | tf_op jit(solution)/shard_map/dot_general | solution.py:20
  232.0 0.7 broadcast_multiply_fusion
  (20 shorter events, 0.5 us)
Async XLA Ops:
  0.6 1.0 copy-start
  69.0 15.4 %all-to-all-start.3 = ((f32[8,128,256]{2,1,0:T(8,128)}), f32[8,128,256]{2,1,0:T(8,128)S(1)}, u32[]{:S(2)}, u32[]{:S(2)}) async-start(f32[8,128,256]{2,1,0:T(8,128)} %broadcast_in_dim.20), calls=%async_computation.3 | async-start | bytes 2097152 | tf_op jit(solution)/shard_map/all_to_all | solution.py:109
  133.7 16.6 %all-to-all-start.7 = ((f32[8,16,256]{2,1,0:T(8,128)}), f32[8,16,256]{2,1,0:T(8,128)S(1)}, u32[]{:S(2)}, u32[]{:S(2)}) async-start(f32[8,16,256]{2,1,0:T(8,128)} %bitcast.8), calls=%async_computation.7 | async-start | bytes 262144 | tf_op jit(solution)/shard_map/all_to_all | solution.py:109

commit v3 on v2

v3 whole, which is shorter than its diff:
```python
import jax
import jax.numpy as jnp
from jax import lax
from jax.experimental import pallas as pl
from jax.experimental.pallas import tpu as pltpu
from jax.sharding import Mesh, PartitionSpec as P

M = 8192
NEAR = ("y", "z_low")
FAR = "z_high"
ROWS = ("inner", "outer")
STEP = 8
LANES = 128
BLOCK = 32
PANEL = 2


def dot(left, right, dims):
    return lax.dot_general(
        left,
        right,
        (dims, ((), ())),
        precision=lax.Precision.HIGHEST,
        preferred_element_type=jnp.float32,
    )


def factor_rows(tiles, first):
    depth = len(tiles)
    row = lax.broadcasted_iota(jnp.int32, (STEP, LANES), 0)
    roots = []
    for panel in range(0, depth, PANEL):
        columns = []
        for i in range(STEP * PANEL):
            tile, lane = divmod(first + panel * STEP + i, LANES)
            columns.append(
                [
                    jnp.broadcast_to(tiles[s][tile][:, lane : lane + 1], (STEP, LANES))
                    for s in range(panel + i // STEP, depth)
                ]
            )
        scales = [jnp.zeros((STEP, LANES), jnp.float32) for _ in range(PANEL)]
        for i in range(STEP * PANEL):
            p, at = divmod(i, STEP)
            root = lax.rsqrt(columns[i][0][at : at + 1, :])
            inverse = root * root
            scales[p] = jnp.where(row == at, root, scales[p])
            weights = [column * inverse for column in columns[i]]
            weights[0] = jnp.where(row > at, weights[0], 0.0)
            for j in range(i + 1, STEP * PANEL):
                q, other = divmod(j, STEP)
                partner = columns[i][q - p][other : other + 1, :]
                columns[j] = [c - w * partner for c, w in zip(columns[j], weights[q - p :])]
            for t in range(len(tiles[panel])):
                source = tiles[panel + p][t][at : at + 1, :]
                for s in range(panel + p, depth):
                    tiles[s][t] = tiles[s][t] - weights[s - panel - p] * source
        roots += scales
    return [[tile * roots[s] for tile in tiles[s]] for s in range(depth)]


def invert_factor(gram, out_ref, work_ref):
    size = gram.shape[0]
    rows = lax.broadcasted_iota(jnp.int32, (size, size), 0)
    lanes = lax.broadcasted_iota(jnp.int32, (size, size), 1)
    work_ref[:, :size] = gram
    work_ref[:, size:] = jnp.where(rows == lanes, 1.0, 0.0).astype(jnp.float32)
    for start in range(0, size, BLOCK):
        rest = start + BLOCK
        low = start // LANES * LANES
        high = size + -(-rest // LANES) * LANES
        tiles = [
            [
                work_ref[pl.ds(start + s, STEP), pl.ds(t, LANES)]
                for t in range(low, high, LANES)
            ]
            for s in range(0, BLOCK, STEP)
        ]
        tiles = factor_rows(tiles, start - low)
        whole = jnp.concatenate([jnp.concatenate(r, axis=1) for r in tiles], axis=0)
        out_ref[pl.ds(start, BLOCK), : high - size] = whole[:, size - low :]
        if high < 2 * size:
            out_ref[pl.ds(start, BLOCK), high - size :] = jnp.zeros(
                (BLOCK, 2 * size - high), jnp.float32
            )
        if rest < size:
            base = rest // LANES * LANES
            left = whole[:, base - low : size - low].T[rest - base :, :]
            work_ref[pl.ds(rest, size - rest), pl.ds(low, high - low)] -= dot(
                left, whole, ((1,), (0,))
            )


def inverse_kernel(sums_ref, inverse_ref, work_ref):
    invert_factor(sums_ref[: inverse_ref.shape[0], :], inverse_ref, work_ref)


def projection_kernel(sums_ref, inverse_ref, coefficients_ref, work_ref):
    size = inverse_ref.shape[0]
    invert_factor(sums_ref[:size, :], inverse_ref, work_ref)
    projection = dot(inverse_ref[...], sums_ref[size:, :], ((1,), (1,)))
    mean = jnp.sum(projection * projection, axis=0, keepdims=True) / size
    coefficients_ref[...] = projection * lax.rsqrt(mean + 1e-06)


def on_sums(kernel, sums, others):
    rank = sums.shape[1]
    vmem = pl.BlockSpec(memory_space=pltpu.VMEM)
    shapes = [(rank, rank), *others]
    return pl.pallas_call(
        kernel,
        out_shape=[jax.ShapeDtypeStruct(shape, jnp.float32) for shape in shapes],
        in_specs=[vmem],
        out_specs=[vmem] * len(shapes),
        scratch_shapes=[pltpu.VMEM((rank, 2 * rank), jnp.float32)],
        cost_estimate=pl.CostEstimate(
            flops=2_000_000_000, transcendentals=rank, bytes_accessed=8 * rank * rank
        ),
        name=kernel.__name__,
    )(sums)


def exchange(tiles, axis):
    return lax.all_to_all(tiles, axis, 0, 0, tiled=True)


def tiles_for(array, axis):
    return array.reshape(lax.axis_size(axis), -1, array.shape[-1])


def copies_for(array, axis):
    return jnp.broadcast_to(array[None], (lax.axis_size(axis), *array.shape))


def scatter_sum(array, axis):
    return exchange(tiles_for(array, axis), axis).sum(axis=0)


def gather(array, axis):
    return exchange(copies_for(array, axis), axis).reshape(-1, array.shape[-1])


def sum_over_rows(array):
    return gather(scatter_sum(array, ROWS), ROWS)


def sums_with(matrix, sample):
    gram = dot(sample, sample, ((0,), (0,)))
    products = dot(matrix, sample, ((0,), (0,)))
    return sum_over_rows(jnp.concatenate([gram, products], axis=0))


def per_device(matrix, sketch):
    rank = sketch.shape[1]
    width = matrix.shape[1]

    partial = dot(matrix, sketch, ((1,), (0,)))
    own = scatter_sum(scatter_sum(partial, NEAR), FAR)
    first = gather(gather(own, FAR), NEAR)

    sums = sums_with(matrix, first)
    (inverse,) = on_sums(inverse_kernel, sums, [])
    partial = dot(matrix, sums[rank:], ((1,), (0,)))
    own = scatter_sum(scatter_sum(partial, NEAR), FAR)
    own = dot(own, inverse, ((1,), (1,)))
    second = gather(gather(own, FAR), NEAR)

    sums = sums_with(matrix, second)
    inverse, coefficients = on_sums(projection_kernel, sums, [(rank, width)])
    basis = dot(second, inverse, ((1,), (1,)))
    return (basis * jnp.sqrt(jnp.float32(M)), coefficients)


def solution(mesh):
    columns, inner, outer = mesh.devices.shape
    split = Mesh(
        mesh.devices.reshape(4, columns // 8, 2, inner, outer),
        ("y", "z_high", "z_low", "inner", "outer"),
    )
    column = ("y", "z_high", "z_low")
    return jax.shard_map(
        per_device,
        mesh=split,
        in_specs=(P(ROWS, column), P(column, None)),
        out_specs=(P(ROWS, None), P(None, column)),
        check_vma=False,
    )
```

time: 234 us -> 229 us (0.979)
  blocking collectives: 171 us -> 186 us
  waiting for transfers between devices: 14.3 us -> 3.82 us
  starting transfers between devices: 7.11 us -> 3.37 us
    all_to_all x10 -> x11, blocking collectives: 171 us -> 186 us  [exchange(): return lax.all_to_all(tiles, axis, 0, 0, tiled=True)]
    all_to_all x2 -> x1, waiting for transfers between devices: 14.3 us -> 3.82 us  [exchange(): return lax.all_to_all(tiles, axis, 0, 0, tiled=True)]
    all_to_all x2 -> x1, starting transfers between devices: 7.11 us -> 3.37 us  [exchange(): return lax.all_to_all(tiles, axis, 0, 0, tiled=True)]
    dot_general x9 -> x8, matrix products: 14.1 us -> 12.8 us  [dot(): lax.dot_general(left, right, (dims, ((), ())), precision=lax.Precision.HI...]
  transfers between devices with their start and end apart: 2 -> 1, of which waited for: 2 -> 1; matrix products, arithmetic and copies ran while one was open for 0% -> 0% of each run, Pallas kernels for 4% -> 4%
where the time goes in v3:
time: 229 us; the launch traced here: 228 us
  blocking collectives  186 us (81%)
  Pallas kernels  19 us (8%)
  matrix products  12.8 us (6%)
  waiting for transfers between devices  3.82 us (2%)
  starting transfers between devices  3.37 us (1%)
    all_to_all x11, blocking collectives, exchange(): return lax.all_to_all(tiles, axis, 0, 0, tiled=True)  186 us
    pallas_call x2, Pallas kernels, on_sums(): pl.pallas_call(kernel, out_shape=[jax.ShapeDtypeStruct(shape, jnp.float32...  19 us
    dot_general x8, matrix products, dot(): lax.dot_general(left, right, (dims, ((), ())), precision=lax.Precision.HI...  12.8 us
  transfers between devices with their start and end apart: 1, of which 1 were waited for; matrix products, arithmetic and copies ran while one was open for 0% of the time, Pallas kernels for 4%

profile of v3, /device:TPU:1, one launch (start us, length us, event | category | flops | bytes accessed | tf_op | source)
XLA Modules:
  0.0 228.0 jit_solution(4832631607430115095)
XLA Ops:
  0.6 0.0 copy-start
  0.6 1.0 copy-done
  1.7 1.9 fusion.1
  3.6 18.9 %all_to_all.60 = f32[8,128,256]{2,1,0:T(8,128)S(1)} all-to-all(f32[8,128,256]{2,1,0:T(8,128)S(1)} %bitcast.44), channel_id=1, replica_groups=mesh['y'=4,'z_high'=8,'z_low'=2,'inner'=2,'outer'=4] {'y','z_low'}, dimensions={0} | all-to-all | bytes 2097152 | tf_op jit(solution)/shard_map/all_to_all | solution.py:124
  22.4 0.1 reduce_sum.54
  22.5 28.9 %all_to_all.61 = f32[8,16,256]{2,1,0:T(8,128)S(1)} all-to-all(f32[8,16,256]{2,1,0:T(8,128)S(1)} %bitcast.49), channel_id=1, replica_groups=mesh['y'=4,'z_high'=8,'z_low'=2,'inner'=2,'outer'=4] {'z_high'}, dimensions={0} | all-to-all | bytes 262144 | tf_op jit(solution)/shard_map/all_to_all | solution.py:124
  51.5 16.5 %all_to_all.62 = f32[8,16,256]{2,1,0:T(8,128)S(1)} all-to-all(f32[8,16,256]{2,1,0:T(8,128)S(1)} %broadcast_in_dim.16), channel_id=1, replica_groups=mesh['y'=4,'z_high'=8,'z_low'=2,'inner'=2,'outer'=4] {'z_high'}, dimensions={0} | all-to-all | bytes 262144 | tf_op jit(solution)/shard_map/all_to_all | solution.py:124
  67.9 0.1 broadcast_in_dim.18
  68.0 14.2 %all_to_all.63 = f32[8,128,256]{2,1,0:T(8,128)S(1)} all-to-all(f32[8,128,256]{2,1,0:T(8,128)S(1)} %broadcast_in_dim.18), channel_id=1, replica_groups=mesh['y'=4,'z_high'=8,'z_low'=2,'inner'=2,'outer'=4] {'y','z_low'}, dimensions={0} | all-to-all | bytes 2097152 | tf_op jit(solution)/shard_map/all_to_all | solution.py:124
  82.2 1.0 convolution_bitcast_fusion.4
  83.2 1.8 convolution_bitcast_fusion.2
  85.1 17.0 %all_to_all.64 = f32[8,48,256]{2,1,0:T(8,128)S(1)} all-to-all(f32[8,48,256]{2,1,0:T(8,128)S(1)} %bitcast.45), channel_id=1, replica_groups=mesh['y'=4,'z_high'=8,'z_low'=2,'inner'=2,'outer'=4] {'inner','outer'}, dimensions={0} | all-to-all | bytes 786432 | tf_op jit(solution)/shard_map/all_to_all | solution.py:124
  102.2 11.2 %all_to_all.65 = f32[8,48,256]{2,1,0:T(8,128)S(1)} all-to-all(f32[8,48,256]{2,1,0:T(8,128)S(1)} %broadcast_in_dim.19), channel_id=1, replica_groups=mesh['y'=4,'z_high'=8,'z_low'=2,'inner'=2,'outer'=4] {'inner','outer'}, dimensions={0} | all-to-all | bytes 786432 | tf_op jit(solution)/shard_map/all_to_all | solution.py:124
  113.3 1.0 convolution_bitcast_fusion
  114.4 0.1 copy.25
  114.5 17.4 %all_to_all.66 = f32[8,128,256]{1,2,0:T(8,128)S(1)} all-to-all(f32[8,128,256]{1,2,0:T(8,128)S(1)} %bitcast.43), channel_id=1, replica_groups=mesh['y'=4,'z_high'=8,'z_low'=2,'inner'=2,'outer'=4] {'y','z_low'}, dimensions={0} | all-to-all | bytes 2097152 | tf_op jit(solution)/shard_map/all_to_all | solution.py:124
  131.8 0.1 reduce_sum.57
  131.9 0.8 copy.18
  132.6 3.4 %all-to-all-start.7 = ((f32[8,16,256]{2,1,0:T(8,128)}), f32[8,16,256]{2,1,0:T(8,128)S(1)}, u32[]{:S(2)}, u32[]{:S(2)}) async-start(f32[8,16,256]{2,1,0:T(8,128)} %bitcast.9), calls=%async_computation.7 | async-start | bytes 262144 | tf_op jit(solution)/shard_map/all_to_all | solution.py:124
  136.0 9.4 %inverse_kernel.1 = f32[256,256]{1,0:T(8,128)} custom-call(f32[384,256]{1,0:T(8,128)} %bitcast.48), custom_call_target="tpu_custom_call" | custom-call | flops 2000000000 | bytes 524288 | tf_op jit(solution)/shard_map/inverse_kernel/pallas_call | solution.py:110
  145.4 3.8 %all-to-all-done.7 = f32[8,16,256]{2,1,0:T(8,128)S(1)} async-done(((f32[8,16,256]{2,1,0:T(8,128)}), f32[8,16,256]{2,1,0:T(8,128)S(1)}, u32[]{:S(2)}, u32[]{:S(2)}) %all-to-all-start.7) | async-done | bytes 131104 | tf_op jit(solution)/shard_map/all_to_all | solution.py:124
  149.2 1.2 fusion.2
  150.4 0.1 broadcast_in_dim.20
  150.5 20.9 %all_to_all.67 = f32[8,16,256]{2,1,0:T(8,128)S(1)} all-to-all(f32[8,16,256]{2,1,0:T(8,128)S(1)} %broadcast_in_dim.20), channel_id=1, replica_groups=mesh['y'=4,'z_high'=8,'z_low'=2,'inner'=2,'outer'=4] {'z_high'}, dimensions={0} | all-to-all | bytes 262144 | tf_op jit(solution)/shard_map/all_to_all | solution.py:124
  171.4 0.1 broadcast_in_dim.44
  171.5 14.4 %all_to_all.68 = f32[8,128,256]{2,1,0:T(8,128)S(1)} all-to-all(f32[8,128,256]{2,1,0:T(8,128)S(1)} %broadcast_in_dim.44), channel_id=1, replica_groups=mesh['y'=4,'z_high'=8,'z_low'=2,'inner'=2,'outer'=4] {'y','z_low'}, dimensions={0} | all-to-all | bytes 2097152 | tf_op jit(solution)/shard_map/all_to_all | solution.py:124
  185.9 1.0 convolution_bitcast_fusion.3
  187.0 1.8 convolution_bitcast_fusion.1
  188.8 15.1 %all_to_all.69 = f32[8,48,256]{2,1,0:T(8,128)S(1)} all-to-all(f32[8,48,256]{2,1,0:T(8,128)S(1)} %bitcast.46), channel_id=1, replica_groups=mesh['y'=4,'z_high'=8,'z_low'=2,'inner'=2,'outer'=4] {'inner','outer'}, dimensions={0} | all-to-all | bytes 786432 | tf_op jit(solution)/shard_map/all_to_all | solution.py:124
  204.0 11.5 %all_to_all.70 = f32[8,48,256]{2,1,0:T(8,128)} all-to-all(f32[8,48,256]{2,1,0:T(8,128)S(1)} %broadcast_in_dim.45), channel_id=1, replica_groups=mesh['y'=4,'z_high'=8,'z_low'=2,'inner'=2,'outer'=4] {'inner','outer'}, dimensions={0} | all-to-all | bytes 786432 | tf_op jit(solution)/shard_map/all_to_all | solution.py:124
  215.5 9.6 %projection_kernel.1 = (f32[256,256]{1,0:T(8,128)}, f32[256,128]{1,0:T(8,128)}) custom-call(f32[384,256]{1,0:T(8,128)} %bitcast.52), custom_call_target="tpu_custom_call" | custom-call | flops 2000000000 | bytes 524288 | tf_op jit(solution)/shard_map/projection_kernel/pallas_call | solution.py:110
  225.1 2.9 %convolution_multiply_fusion = f32[1024,256]{1,0:T(8,128)} fusion(f32[1024,256]{1,0:T(8,128)S(1)} %bitcast.41, f32[256,256]{1,0:T(8,128)} %get-tuple-element.4), kind=kOutput, calls=%fused_computation.1 | convolution fusion | flops 805568512 | bytes 2359296 | tf_op jit(solution)/shard_map/dot_general | solution.py:19
  (11 shorter events, 0.2 us)
Async XLA Ops:
  0.6 1.0 copy-start
  113.3 1.0 copy-start.1
  132.6 16.6 %all-to-all-start.7 = ((f32[8,16,256]{2,1,0:T(8,128)}), f32[8,16,256]{2,1,0:T(8,128)S(1)}, u32[]{:S(2)}, u32[]{:S(2)}) async-start(f32[8,16,256]{2,1,0:T(8,128)} %bitcast.9), calls=%async_computation.7 | async-start | bytes 262144 | tf_op jit(solution)/shard_map/all_to_all | solution.py:124

commit v4 on v3

--- a/solution.py
+++ b/solution.py
@@ -13,6 +13,7 @@
 LANES = 128
 BLOCK = 32
 PANEL = 2
+CHUNKS = 4
 
 
 def dot(left, right, dims):
@@ -59,13 +60,19 @@
     return [[tile * roots[s] for tile in tiles[s]] for s in range(depth)]
 
 
-def invert_factor(gram, out_ref, work_ref):
-    size = gram.shape[0]
+def invert_factor(sums_ref, out_ref, work_ref, between=None):
+    size = out_ref.shape[0]
+    half = size // 2
     rows = lax.broadcasted_iota(jnp.int32, (size, size), 0)
     lanes = lax.broadcasted_iota(jnp.int32, (size, size), 1)
-    work_ref[:, :size] = gram
+    work_ref[half:, :size] = sums_ref[:half, :]
+    work_ref[: half // 2, :half] = sums_ref[half : half + half // 2, :half]
+    work_ref[half // 2 : half, :half] = sums_ref[half : half + half // 2, half:]
+    work_ref[:half, half:size] = sums_ref[:half, :half].T
     work_ref[:, size:] = jnp.where(rows == lanes, 1.0, 0.0).astype(jnp.float32)
     for start in range(0, size, BLOCK):
+        if between is not None:
+            between(start)
         rest = start + BLOCK
         low = start // LANES * LANES
         high = size + -(-rest // LANES) * LANES
@@ -91,33 +98,90 @@
             )
 
 
-def inverse_kernel(sums_ref, inverse_ref, work_ref):
-    invert_factor(sums_ref[: inverse_ref.shape[0], :], inverse_ref, work_ref)
-
-
-def projection_kernel(sums_ref, inverse_ref, coefficients_ref, work_ref):
+def result_kernel(
+    sums_ref, sample_ref, basis_ref, coefficients_ref,
+    inverse_ref, work_ref, left_ref, right_ref, in_sem, out_sems,
+):
     size = inverse_ref.shape[0]
-    invert_factor(sums_ref[:size, :], inverse_ref, work_ref)
-    projection = dot(inverse_ref[...], sums_ref[size:, :], ((1,), (1,)))
+    half = size // 2
+    count = sample_ref.shape[0]
+    arriving = pltpu.make_async_copy(sample_ref, left_ref, in_sem)
+    arriving.start()
+    share = count // (half // BLOCK)
+
+    def low_half(start):
+        if start == half:
+            arriving.wait()
+        if start >= half:
+            rows = pl.ds((start - half) // BLOCK * share, share)
+            low = dot(left_ref[rows, :half], inverse_ref[:half, :half], ((1,), (1,)))
+            right_ref[rows, :half] = low * M**0.5
+
+    invert_factor(sums_ref, inverse_ref, work_ref, low_half)
+    leaving = []
+    for index, start in enumerate(range(0, count, count // CHUNKS)):
+        part = pl.ds(start, count // CHUNKS)
+        high = dot(left_ref[part, :], inverse_ref[half:, :], ((1,), (1,)))
+        right_ref[part, half:] = high * M**0.5
+        leaving.append(
+            pltpu.make_async_copy(right_ref.at[part], basis_ref.at[part], out_sems.at[index])
+        )
+        leaving[-1].start()
+    products = sums_ref[half + half // 2 :, :]
+    projection = dot(inverse_ref[...], products, ((1,), (1,)))
     mean = jnp.sum(projection * projection, axis=0, keepdims=True) / size
     coefficients_ref[...] = projection * lax.rsqrt(mean + 1e-06)
-
-
-def on_sums(kernel, sums, others):
+    for copy in leaving:
+        copy.wait()
+
+
+def work_for(rank):
+    return pltpu.VMEM((rank, 2 * rank), jnp.float32)
+
+
+def price_of(rank):
+    return pl.CostEstimate(
+        flops=2_000_000_000, transcendentals=rank, bytes_accessed=8 * rank * rank
+    )
+
+
+def inverse_factor(sums):
     rank = sums.shape[1]
     vmem = pl.BlockSpec(memory_space=pltpu.VMEM)
-    shapes = [(rank, rank), *others]
     return pl.pallas_call(
-        kernel,
-        out_shape=[jax.ShapeDtypeStruct(shape, jnp.float32) for shape in shapes],
+        invert_factor,
+        out_shape=jax.ShapeDtypeStruct((rank, rank), jnp.float32),
         in_specs=[vmem],
-        out_specs=[vmem] * len(shapes),
-        scratch_shapes=[pltpu.VMEM((rank, 2 * rank), jnp.float32)],
-        cost_estimate=pl.CostEstimate(
-            flops=2_000_000_000, transcendentals=rank, bytes_accessed=8 * rank * rank
-        ),
-        name=kernel.__name__,
+        out_specs=vmem,
+        scratch_shapes=[work_for(rank)],
+        cost_estimate=price_of(rank),
+        name="inverse_factor",
     )(sums)
+
+
+def results(sums, sample, width):
+    rank = sums.shape[1]
+    vmem = pl.BlockSpec(memory_space=pltpu.VMEM)
+    anywhere = pl.BlockSpec(memory_space=pl.ANY)
+    return pl.pallas_call(
+        result_kernel,
+        out_shape=[
+            jax.ShapeDtypeStruct(sample.shape, jnp.float32),
+            jax.ShapeDtypeStruct((rank, width), jnp.float32),
+        ],
+        in_specs=[vmem, anywhere],
+        out_specs=[anywhere, vmem],
+        scratch_shapes=[
+            pltpu.VMEM((rank, rank), jnp.float32),
+            work_for(rank),
+            pltpu.VMEM(sample.shape, jnp.float32),
+            pltpu.VMEM(sample.shape, jnp.float32),
+            pltpu.SemaphoreType.DMA(()),
+            pltpu.SemaphoreType.DMA((CHUNKS,)),
+        ],
+        cost_estimate=price_of(rank),
+        name="results",
+    )(sums, sample)
 
 
 def exchange(tiles, axis):
@@ -145,13 +209,15 @@
 
 
 def sums_with(matrix, sample):
-    gram = dot(sample, sample, ((0,), (0,)))
+    half = sample.shape[1] // 2
+    lower = dot(sample[:, half:], sample, ((0,), (0,)))
+    corner = dot(sample[:, :half], sample[:, :half], ((0,), (0,)))
+    corner = jnp.concatenate([corner[: half // 2], corner[half // 2 :]], axis=1)
     products = dot(matrix, sample, ((0,), (0,)))
-    return sum_over_rows(jnp.concatenate([gram, products], axis=0))
+    return sum_over_rows(jnp.concatenate([lower, corner, products], axis=0))
 
 
 def per_device(matrix, sketch):
-    rank = sketch.shape[1]
     width = matrix.shape[1]
 
     partial = dot(matrix, sketch, ((1,), (0,)))
@@ -159,16 +225,13 @@
     first = gather(gather(own, FAR), NEAR)
 
     sums = sums_with(matrix, first)
-    (inverse,) = on_sums(inverse_kernel, sums, [])
-    partial = dot(matrix, sums[rank:], ((1,), (0,)))
+    inverse = inverse_factor(sums)
+    partial = dot(matrix, sums[-width:], ((1,), (0,)))
     own = scatter_sum(scatter_sum(partial, NEAR), FAR)
     own = dot(own, inverse, ((1,), (1,)))
     second = gather(gather(own, FAR), NEAR)
 
-    sums = sums_with(matrix, second)
-    inverse, coefficients = on_sums(projection_kernel, sums, [(rank, width)])
-    basis = dot(second, inverse, ((1,), (1,)))
-    return (basis * jnp.sqrt(jnp.float32(M)), coefficients)
+    return tuple(results(sums_with(matrix, second), second, width))
 
 
 def solution(mesh):

time: 229 us -> 226 us (0.987)
  matrix products: 12.8 us -> 10.2 us
    dot_general x8 -> x9, matrix products: 12.8 us -> 10.2 us  [dot(): lax.dot_general(left, right, (dims, ((), ())), precision=lax.Precision.HI...]
where the time goes in v4:
time: 226 us; the launch traced here: 225 us
  blocking collectives  184 us (81%)
  Pallas kernels  20.8 us (9%)
  matrix products  10.2 us (5%)
  waiting for transfers between devices  3.77 us (2%)
  starting transfers between devices  3.55 us (2%)
    all_to_all x11, blocking collectives, exchange(): return lax.all_to_all(tiles, axis, 0, 0, tiled=True)  184 us
    pallas_call x1, Pallas kernels, results(): pl.pallas_call(result_kernel, out_shape=[jax.ShapeDtypeStruct(sample.shap...  11.5 us
    dot_general x9, matrix products, dot(): lax.dot_general(left, right, (dims, ((), ())), precision=lax.Precision.HI...  10.2 us
    pallas_call x1, Pallas kernels, inverse_factor(): pl.pallas_call(invert_factor, out_shape=jax.ShapeDtypeStruct((rank, rank)...  9.32 us
  transfers between devices with their start and end apart: 1, of which 1 were waited for; matrix products, arithmetic and copies ran while one was open for 0% of the time, Pallas kernels for 4%

profile of v4, /device:TPU:1, one launch (start us, length us, event | category | flops | bytes accessed | tf_op | source)
XLA Modules:
  0.0 225.5 jit_solution(275916019360768167)
XLA Ops:
  0.6 1.0 copy-done
  1.7 1.9 fusion.11
  3.6 18.9 %all_to_all.60 = f32[8,128,256]{2,1,0:T(8,128)S(1)} all-to-all(f32[8,128,256]{2,1,0:T(8,128)S(1)} %bitcast.40), channel_id=1, replica_groups=mesh['y'=4,'z_high'=8,'z_low'=2,'inner'=2,'outer'=4] {'y','z_low'}, dimensions={0} | all-to-all | bytes 2097152 | tf_op jit(solution)/shard_map/all_to_all | solution.py:188
  22.4 0.1 reduce_sum.54
  22.5 28.9 %all_to_all.61 = f32[8,16,256]{2,1,0:T(8,128)S(1)} all-to-all(f32[8,16,256]{2,1,0:T(8,128)S(1)} %bitcast.45), channel_id=1, replica_groups=mesh['y'=4,'z_high'=8,'z_low'=2,'inner'=2,'outer'=4] {'z_high'}, dimensions={0} | all-to-all | bytes 262144 | tf_op jit(solution)/shard_map/all_to_all | solution.py:188
  51.5 16.5 %all_to_all.62 = f32[8,16,256]{2,1,0:T(8,128)S(1)} all-to-all(f32[8,16,256]{2,1,0:T(8,128)S(1)} %broadcast_in_dim.16), channel_id=1, replica_groups=mesh['y'=4,'z_high'=8,'z_low'=2,'inner'=2,'outer'=4] {'z_high'}, dimensions={0} | all-to-all | bytes 262144 | tf_op jit(solution)/shard_map/all_to_all | solution.py:188
  67.9 0.1 broadcast_in_dim.18
  68.0 14.2 %all_to_all.63 = f32[8,128,256]{2,1,0:T(8,128)S(1)} all-to-all(f32[8,128,256]{2,1,0:T(8,128)S(1)} %broadcast_in_dim.18), channel_id=1, replica_groups=mesh['y'=4,'z_high'=8,'z_low'=2,'inner'=2,'outer'=4] {'y','z_low'}, dimensions={0} | all-to-all | bytes 2097152 | tf_op jit(solution)/shard_map/all_to_all | solution.py:188
  82.2 1.0 fusion.4
  83.2 1.0 fusion.6
  84.2 1.0 convolution_bitcast_fusion.2
  85.3 16.6 %all_to_all.64 = f32[8,40,256]{2,1,0:T(8,128)S(1)} all-to-all(f32[8,40,256]{2,1,0:T(8,128)S(1)} %bitcast.41), channel_id=1, replica_groups=mesh['y'=4,'z_high'=8,'z_low'=2,'inner'=2,'outer'=4] {'inner','outer'}, dimensions={0} | all-to-all | bytes 655360 | tf_op jit(solution)/shard_map/all_to_all | solution.py:188
  101.9 10.5 %all_to_all.65 = f32[8,40,256]{2,1,0:T(8,128)S(1)} all-to-all(f32[8,40,256]{2,1,0:T(8,128)S(1)} %broadcast_in_dim.19), channel_id=1, replica_groups=mesh['y'=4,'z_high'=8,'z_low'=2,'inner'=2,'outer'=4] {'inner','outer'}, dimensions={0} | all-to-all | bytes 655360 | tf_op jit(solution)/shard_map/all_to_all | solution.py:188
  112.4 1.0 convolution_bitcast_fusion
  113.4 0.1 copy.15
  113.5 17.4 %all_to_all.66 = f32[8,128,256]{1,2,0:T(8,128)S(1)} all-to-all(f32[8,128,256]{1,2,0:T(8,128)S(1)} %bitcast.39), channel_id=1, replica_groups=mesh['y'=4,'z_high'=8,'z_low'=2,'inner'=2,'outer'=4] {'y','z_low'}, dimensions={0} | all-to-all | bytes 2097152 | tf_op jit(solution)/shard_map/all_to_all | solution.py:188
  130.9 0.1 reduce_sum.57
  130.9 0.8 copy.11
  131.7 3.6 %all-to-all-start.7 = ((f32[8,16,256]{2,1,0:T(8,128)}), f32[8,16,256]{2,1,0:T(8,128)S(1)}, u32[]{:S(2)}, u32[]{:S(2)}) async-start(f32[8,16,256]{2,1,0:T(8,128)} %bitcast.8), calls=%async_computation.7 | async-start | bytes 262144 | tf_op jit(solution)/shard_map/all_to_all | solution.py:188
  135.3 9.3 %inverse_factor.1 = f32[256,256]{1,0:T(8,128)} custom-call(f32[320,256]{1,0:T(8,128)} %bitcast.44), custom_call_target="tpu_custom_call" | custom-call | flops 2000000000 | bytes 524288 | tf_op jit(solution)/shard_map/inverse_factor/pallas_call | solution.py:151
  144.6 3.8 %all-to-all-done.7 = f32[8,16,256]{2,1,0:T(8,128)S(1)} async-done(((f32[8,16,256]{2,1,0:T(8,128)}), f32[8,16,256]{2,1,0:T(8,128)S(1)}, u32[]{:S(2)}, u32[]{:S(2)}) %all-to-all-start.7) | async-done | bytes 131104 | tf_op jit(solution)/shard_map/all_to_all | solution.py:188
  148.4 1.2 fusion.12
  149.6 0.1 broadcast_in_dim.20
  149.7 20.8 %all_to_all.67 = f32[8,16,256]{2,1,0:T(8,128)S(1)} all-to-all(f32[8,16,256]{2,1,0:T(8,128)S(1)} %broadcast_in_dim.20), channel_id=1, replica_groups=mesh['y'=4,'z_high'=8,'z_low'=2,'inner'=2,'outer'=4] {'z_high'}, dimensions={0} | all-to-all | bytes 262144 | tf_op jit(solution)/shard_map/all_to_all | solution.py:188
  170.4 0.1 broadcast_in_dim.44
  170.5 14.4 %all_to_all.68 = f32[8,128,256]{2,1,0:T(8,128)S(1)} all-to-all(f32[8,128,256]{2,1,0:T(8,128)S(1)} %broadcast_in_dim.44), channel_id=1, replica_groups=mesh['y'=4,'z_high'=8,'z_low'=2,'inner'=2,'outer'=4] {'y','z_low'}, dimensions={0} | all-to-all | bytes 2097152 | tf_op jit(solution)/shard_map/all_to_all | solution.py:188
  185.0 1.0 fusion
  186.0 1.0 convolution_bitcast_fusion.1
  187.0 1.0 fusion.2
  188.1 14.6 %all_to_all.69 = f32[8,40,256]{2,1,0:T(8,128)S(1)} all-to-all(f32[8,40,256]{2,1,0:T(8,128)S(1)} %bitcast.42), channel_id=1, replica_groups=mesh['y'=4,'z_high'=8,'z_low'=2,'inner'=2,'outer'=4] {'inner','outer'}, dimensions={0} | all-to-all | bytes 655360 | tf_op jit(solution)/shard_map/all_to_all | solution.py:188
  202.8 11.0 %all_to_all.70 = f32[8,40,256]{2,1,0:T(8,128)} all-to-all(f32[8,40,256]{2,1,0:T(8,128)S(1)} %broadcast_in_dim.45), channel_id=1, replica_groups=mesh['y'=4,'z_high'=8,'z_low'=2,'inner'=2,'outer'=4] {'inner','outer'}, dimensions={0} | all-to-all | bytes 655360 | tf_op jit(solution)/shard_map/all_to_all | solution.py:188
  213.8 11.5 %results.1 = (f32[1024,256]{1,0:T(8,128)}, f32[256,128]{1,0:T(8,128)}) custom-call(f32[320,256]{1,0:T(8,128)} %bitcast.48, f32[1024,256]{1,0:T(8,128)} %bitcast.35), custom_call_target="tpu_custom_call" | custom-call | flops 2000000000 | bytes 524288 | tf_op jit(solution)/shard_map/results/pallas_call | solution.py:166
  (16 shorter events, 0.2 us)
Async XLA Ops:
  0.6 1.0 copy-start
  112.4 1.0 copy-start.2
  131.7 16.7 %all-to-all-start.7 = ((f32[8,16,256]{2,1,0:T(8,128)}), f32[8,16,256]{2,1,0:T(8,128)S(1)}, u32[]{:S(2)}, u32[]{:S(2)}) async-start(f32[8,16,256]{2,1,0:T(8,128)} %bitcast.8), calls=%async_computation.7 | async-start | bytes 262144 | tf_op jit(solution)/shard_map/all_to_all | solution.py:188
  185.0 2.0 copy-start.1

commit v5 on v4

--- a/solution.py
+++ b/solution.py
@@ -6,9 +6,10 @@
 from jax.sharding import Mesh, PartitionSpec as P
 
 M = 8192
-NEAR = ("y", "z_low")
+NEAR = ("z_low", "y")
 FAR = "z_high"
 ROWS = ("inner", "outer")
+PEERS = ("outer", "inner")
 STEP = 8
 LANES = 128
 BLOCK = 32
@@ -205,7 +206,7 @@
 
 
 def sum_over_rows(array):
-    return gather(scatter_sum(array, ROWS), ROWS)
+    return gather(scatter_sum(array, PEERS), PEERS)
 
 
 def sums_with(matrix, sample):

time: 226 us -> 225 us (level)
  no operation moved by 1% of the time
where the time goes in v5:
time: 225 us; the launch traced here: 224 us
  blocking collectives  182 us (81%)
  Pallas kernels  20.8 us (9%)
  matrix products  10.2 us (5%)
  waiting for transfers between devices  4.42 us (2%)
  starting transfers between devices  3.55 us (2%)
    all_to_all x11, blocking collectives, exchange(): return lax.all_to_all(tiles, axis, 0, 0, tiled=True)  182 us
    pallas_call x1, Pallas kernels, results(): pl.pallas_call(result_kernel, out_shape=[jax.ShapeDtypeStruct(sample.shap...  11.5 us
    dot_general x9, matrix products, dot(): lax.dot_general(left, right, (dims, ((), ())), precision=lax.Precision.HI...  10.2 us
    pallas_call x1, Pallas kernels, inverse_factor(): pl.pallas_call(invert_factor, out_shape=jax.ShapeDtypeStruct((rank, rank)...  9.32 us
  transfers between devices with their start and end apart: 1, of which 1 were waited for; matrix products, arithmetic and copies ran while one was open for 0% of the time, Pallas kernels for 4%

profile of v5, /device:TPU:1, one launch (start us, length us, event | category | flops | bytes accessed | tf_op | source)
XLA Modules:
  0.0 224.3 jit_solution(16170509309775122719)
XLA Ops:
  0.6 1.0 copy-done
  1.7 1.9 fusion.11
  3.6 17.9 %all_to_all.60 = f32[8,128,256]{2,1,0:T(8,128)S(1)} all-to-all(f32[8,128,256]{2,1,0:T(8,128)S(1)} %bitcast.40), channel_id=1, replica_groups=mesh['y'=4,'z_high'=8,'z_low'=2,'inner'=2,'outer'=4] {'z_low','y'}, dimensions={0} | all-to-all | bytes 2097152 | tf_op jit(solution)/shard_map/all_to_all | solution.py:189
  21.4 0.1 reduce_sum.54
  21.5 29.9 %all_to_all.61 = f32[8,16,256]{2,1,0:T(8,128)S(1)} all-to-all(f32[8,16,256]{2,1,0:T(8,128)S(1)} %bitcast.45), channel_id=1, replica_groups=mesh['y'=4,'z_high'=8,'z_low'=2,'inner'=2,'outer'=4] {'z_high'}, dimensions={0} | all-to-all | bytes 262144 | tf_op jit(solution)/shard_map/all_to_all | solution.py:189
  51.4 15.7 %all_to_all.62 = f32[8,16,256]{2,1,0:T(8,128)S(1)} all-to-all(f32[8,16,256]{2,1,0:T(8,128)S(1)} %broadcast_in_dim.16), channel_id=1, replica_groups=mesh['y'=4,'z_high'=8,'z_low'=2,'inner'=2,'outer'=4] {'z_high'}, dimensions={0} | all-to-all | bytes 262144 | tf_op jit(solution)/shard_map/all_to_all | solution.py:189
  67.1 0.1 broadcast_in_dim.18
  67.2 12.9 %all_to_all.63 = f32[8,128,256]{2,1,0:T(8,128)S(1)} all-to-all(f32[8,128,256]{2,1,0:T(8,128)S(1)} %broadcast_in_dim.18), channel_id=1, replica_groups=mesh['y'=4,'z_high'=8,'z_low'=2,'inner'=2,'outer'=4] {'z_low','y'}, dimensions={0} | all-to-all | bytes 2097152 | tf_op jit(solution)/shard_map/all_to_all | solution.py:189
  80.1 1.0 fusion.4
  81.1 1.0 fusion.6
  82.1 1.0 convolution_bitcast_fusion.2
  83.2 17.8 %all_to_all.64 = f32[8,40,256]{2,1,0:T(8,128)S(1)} all-to-all(f32[8,40,256]{2,1,0:T(8,128)S(1)} %bitcast.41), channel_id=1, replica_groups=mesh['y'=4,'z_high'=8,'z_low'=2,'inner'=2,'outer'=4] {'outer','inner'}, dimensions={0} | all-to-all | bytes 655360 | tf_op jit(solution)/shard_map/all_to_all | solution.py:189
  101.0 10.6 %all_to_all.65 = f32[8,40,256]{2,1,0:T(8,128)S(1)} all-to-all(f32[8,40,256]{2,1,0:T(8,128)S(1)} %broadcast_in_dim.19), channel_id=1, replica_groups=mesh['y'=4,'z_high'=8,'z_low'=2,'inner'=2,'outer'=4] {'outer','inner'}, dimensions={0} | all-to-all | bytes 655360 | tf_op jit(solution)/shard_map/all_to_all | solution.py:189
  111.6 1.0 convolution_bitcast_fusion
  112.7 0.1 copy.15
  112.7 16.8 %all_to_all.66 = f32[8,128,256]{1,2,0:T(8,128)S(1)} all-to-all(f32[8,128,256]{1,2,0:T(8,128)S(1)} %bitcast.39), channel_id=1, replica_groups=mesh['y'=4,'z_high'=8,'z_low'=2,'inner'=2,'outer'=4] {'z_low','y'}, dimensions={0} | all-to-all | bytes 2097152 | tf_op jit(solution)/shard_map/all_to_all | solution.py:189
  129.5 0.1 reduce_sum.57
  129.6 0.8 copy.11
  130.3 3.6 %all-to-all-start.7 = ((f32[8,16,256]{2,1,0:T(8,128)}), f32[8,16,256]{2,1,0:T(8,128)S(1)}, u32[]{:S(2)}, u32[]{:S(2)}) async-start(f32[8,16,256]{2,1,0:T(8,128)} %bitcast.8), calls=%async_computation.7 | async-start | bytes 262144 | tf_op jit(solution)/shard_map/all_to_all | solution.py:189
  133.9 9.3 %inverse_factor.1 = f32[256,256]{1,0:T(8,128)} custom-call(f32[320,256]{1,0:T(8,128)} %bitcast.44), custom_call_target="tpu_custom_call" | custom-call | flops 2000000000 | bytes 524288 | tf_op jit(solution)/shard_map/inverse_factor/pallas_call | solution.py:152
  143.2 4.4 %all-to-all-done.7 = f32[8,16,256]{2,1,0:T(8,128)S(1)} async-done(((f32[8,16,256]{2,1,0:T(8,128)}), f32[8,16,256]{2,1,0:T(8,128)S(1)}, u32[]{:S(2)}, u32[]{:S(2)}) %all-to-all-start.7) | async-done | bytes 131104 | tf_op jit(solution)/shard_map/all_to_all | solution.py:189
  147.6 1.2 fusion.12
  148.9 0.1 broadcast_in_dim.20
  148.9 20.2 %all_to_all.67 = f32[8,16,256]{2,1,0:T(8,128)S(1)} all-to-all(f32[8,16,256]{2,1,0:T(8,128)S(1)} %broadcast_in_dim.20), channel_id=1, replica_groups=mesh['y'=4,'z_high'=8,'z_low'=2,'inner'=2,'outer'=4] {'z_high'}, dimensions={0} | all-to-all | bytes 262144 | tf_op jit(solution)/shard_map/all_to_all | solution.py:189
  169.1 0.1 broadcast_in_dim.44
  169.2 13.8 %all_to_all.68 = f32[8,128,256]{2,1,0:T(8,128)S(1)} all-to-all(f32[8,128,256]{2,1,0:T(8,128)S(1)} %broadcast_in_dim.44), channel_id=1, replica_groups=mesh['y'=4,'z_high'=8,'z_low'=2,'inner'=2,'outer'=4] {'z_low','y'}, dimensions={0} | all-to-all | bytes 2097152 | tf_op jit(solution)/shard_map/all_to_all | solution.py:189
  183.0 1.0 fusion
  184.0 1.0 convolution_bitcast_fusion.1
  185.1 1.0 fusion.2
  186.2 15.1 %all_to_all.69 = f32[8,40,256]{2,1,0:T(8,128)S(1)} all-to-all(f32[8,40,256]{2,1,0:T(8,128)S(1)} %bitcast.42), channel_id=1, replica_groups=mesh['y'=4,'z_high'=8,'z_low'=2,'inner'=2,'outer'=4] {'outer','inner'}, dimensions={0} | all-to-all | bytes 655360 | tf_op jit(solution)/shard_map/all_to_all | solution.py:189
  201.3 11.3 %all_to_all.70 = f32[8,40,256]{2,1,0:T(8,128)} all-to-all(f32[8,40,256]{2,1,0:T(8,128)S(1)} %broadcast_in_dim.45), channel_id=1, replica_groups=mesh['y'=4,'z_high'=8,'z_low'=2,'inner'=2,'outer'=4] {'outer','inner'}, dimensions={0} | all-to-all | bytes 655360 | tf_op jit(solution)/shard_map/all_to_all | solution.py:189
  212.6 11.5 %results.1 = (f32[1024,256]{1,0:T(8,128)}, f32[256,128]{1,0:T(8,128)}) custom-call(f32[320,256]{1,0:T(8,128)} %bitcast.48, f32[1024,256]{1,0:T(8,128)} %bitcast.35), custom_call_target="tpu_custom_call" | custom-call | flops 2000000000 | bytes 524288 | tf_op jit(solution)/shard_map/results/pallas_call | solution.py:167
  (16 shorter events, 0.2 us)
Async XLA Ops:
  0.6 1.0 copy-start
  111.6 1.0 copy-start.2
  130.3 17.3 %all-to-all-start.7 = ((f32[8,16,256]{2,1,0:T(8,128)}), f32[8,16,256]{2,1,0:T(8,128)S(1)}, u32[]{:S(2)}, u32[]{:S(2)}) async-start(f32[8,16,256]{2,1,0:T(8,128)} %bitcast.8), calls=%async_computation.7 | async-start | bytes 262144 | tf_op jit(solution)/shard_map/all_to_all | solution.py:189
  183.0 2.0 copy-start.1

commit v6 on v4

--- a/solution.py
+++ b/solution.py
@@ -6,7 +6,7 @@
 from jax.sharding import Mesh, PartitionSpec as P
 
 M = 8192
-NEAR = ("y", "z_low")
+NEAR = ("z_low", "y")
 FAR = "z_high"
 ROWS = ("inner", "outer")
 STEP = 8

time: 226 us -> 226 us (level)
  no operation moved by 1% of the time
where the time goes in v6:
time: 226 us; the launch traced here: 225 us
  blocking collectives  183 us (81%)
  Pallas kernels  20.8 us (9%)
  matrix products  10.3 us (5%)
  waiting for transfers between devices  4.39 us (2%)
  starting transfers between devices  3.55 us (2%)
    all_to_all x11, blocking collectives, exchange(): return lax.all_to_all(tiles, axis, 0, 0, tiled=True)  183 us
    pallas_call x1, Pallas kernels, results(): pl.pallas_call(result_kernel, out_shape=[jax.ShapeDtypeStruct(sample.shap...  11.5 us
    dot_general x9, matrix products, dot(): lax.dot_general(left, right, (dims, ((), ())), precision=lax.Precision.HI...  10.3 us
    pallas_call x1, Pallas kernels, inverse_factor(): pl.pallas_call(invert_factor, out_shape=jax.ShapeDtypeStruct((rank, rank)...  9.32 us
  transfers between devices with their start and end apart: 1, of which 1 were waited for; matrix products, arithmetic and copies ran while one was open for 0% of the time, Pallas kernels for 4%

profile of v6, /device:TPU:1, one launch (start us, length us, event | category | flops | bytes accessed | tf_op | source)
XLA Modules:
  0.0 225.3 jit_solution(9607902809308800655)
XLA Ops:
  0.6 1.0 copy-done
  1.7 1.9 fusion.11
  3.6 17.9 %all_to_all.60 = f32[8,128,256]{2,1,0:T(8,128)S(1)} all-to-all(f32[8,128,256]{2,1,0:T(8,128)S(1)} %bitcast.40), channel_id=1, replica_groups=mesh['y'=4,'z_high'=8,'z_low'=2,'inner'=2,'outer'=4] {'z_low','y'}, dimensions={0} | all-to-all | bytes 2097152 | tf_op jit(solution)/shard_map/all_to_all | solution.py:188
  21.4 0.1 reduce_sum.54
  21.5 29.9 %all_to_all.61 = f32[8,16,256]{2,1,0:T(8,128)S(1)} all-to-all(f32[8,16,256]{2,1,0:T(8,128)S(1)} %bitcast.45), channel_id=1, replica_groups=mesh['y'=4,'z_high'=8,'z_low'=2,'inner'=2,'outer'=4] {'z_high'}, dimensions={0} | all-to-all | bytes 262144 | tf_op jit(solution)/shard_map/all_to_all | solution.py:188
  51.4 15.7 %all_to_all.62 = f32[8,16,256]{2,1,0:T(8,128)S(1)} all-to-all(f32[8,16,256]{2,1,0:T(8,128)S(1)} %broadcast_in_dim.16), channel_id=1, replica_groups=mesh['y'=4,'z_high'=8,'z_low'=2,'inner'=2,'outer'=4] {'z_high'}, dimensions={0} | all-to-all | bytes 262144 | tf_op jit(solution)/shard_map/all_to_all | solution.py:188
  67.1 0.1 broadcast_in_dim.18
  67.2 12.9 %all_to_all.63 = f32[8,128,256]{2,1,0:T(8,128)S(1)} all-to-all(f32[8,128,256]{2,1,0:T(8,128)S(1)} %broadcast_in_dim.18), channel_id=1, replica_groups=mesh['y'=4,'z_high'=8,'z_low'=2,'inner'=2,'outer'=4] {'z_low','y'}, dimensions={0} | all-to-all | bytes 2097152 | tf_op jit(solution)/shard_map/all_to_all | solution.py:188
  80.1 1.0 fusion.4
  81.1 1.0 fusion.6
  82.1 1.0 convolution_bitcast_fusion.2
  83.2 17.9 %all_to_all.64 = f32[8,40,256]{2,1,0:T(8,128)S(1)} all-to-all(f32[8,40,256]{2,1,0:T(8,128)S(1)} %bitcast.41), channel_id=1, replica_groups=mesh['y'=4,'z_high'=8,'z_low'=2,'inner'=2,'outer'=4] {'inner','outer'}, dimensions={0} | all-to-all | bytes 655360 | tf_op jit(solution)/shard_map/all_to_all | solution.py:188
  101.1 10.5 %all_to_all.65 = f32[8,40,256]{2,1,0:T(8,128)S(1)} all-to-all(f32[8,40,256]{2,1,0:T(8,128)S(1)} %broadcast_in_dim.19), channel_id=1, replica_groups=mesh['y'=4,'z_high'=8,'z_low'=2,'inner'=2,'outer'=4] {'inner','outer'}, dimensions={0} | all-to-all | bytes 655360 | tf_op jit(solution)/shard_map/all_to_all | solution.py:188
  111.6 1.0 convolution_bitcast_fusion
  112.6 0.1 copy.15
  112.7 16.8 %all_to_all.66 = f32[8,128,256]{1,2,0:T(8,128)S(1)} all-to-all(f32[8,128,256]{1,2,0:T(8,128)S(1)} %bitcast.39), channel_id=1, replica_groups=mesh['y'=4,'z_high'=8,'z_low'=2,'inner'=2,'outer'=4] {'z_low','y'}, dimensions={0} | all-to-all | bytes 2097152 | tf_op jit(solution)/shard_map/all_to_all | solution.py:188
  129.5 0.1 reduce_sum.57
  129.5 0.8 copy.11
  130.3 3.6 %all-to-all-start.7 = ((f32[8,16,256]{2,1,0:T(8,128)}), f32[8,16,256]{2,1,0:T(8,128)S(1)}, u32[]{:S(2)}, u32[]{:S(2)}) async-start(f32[8,16,256]{2,1,0:T(8,128)} %bitcast.8), calls=%async_computation.7 | async-start | bytes 262144 | tf_op jit(solution)/shard_map/all_to_all | solution.py:188
  133.8 9.3 %inverse_factor.1 = f32[256,256]{1,0:T(8,128)} custom-call(f32[320,256]{1,0:T(8,128)} %bitcast.44), custom_call_target="tpu_custom_call" | custom-call | flops 2000000000 | bytes 524288 | tf_op jit(solution)/shard_map/inverse_factor/pallas_call | solution.py:151
  143.2 4.4 %all-to-all-done.7 = f32[8,16,256]{2,1,0:T(8,128)S(1)} async-done(((f32[8,16,256]{2,1,0:T(8,128)}), f32[8,16,256]{2,1,0:T(8,128)S(1)}, u32[]{:S(2)}, u32[]{:S(2)}) %all-to-all-start.7) | async-done | bytes 131104 | tf_op jit(solution)/shard_map/all_to_all | solution.py:188
  147.6 1.2 fusion.12
  148.8 0.1 broadcast_in_dim.20
  148.9 20.2 %all_to_all.67 = f32[8,16,256]{2,1,0:T(8,128)S(1)} all-to-all(f32[8,16,256]{2,1,0:T(8,128)S(1)} %broadcast_in_dim.20), channel_id=1, replica_groups=mesh['y'=4,'z_high'=8,'z_low'=2,'inner'=2,'outer'=4] {'z_high'}, dimensions={0} | all-to-all | bytes 262144 | tf_op jit(solution)/shard_map/all_to_all | solution.py:188
  169.1 0.1 broadcast_in_dim.44
  169.2 15.4 %all_to_all.68 = f32[8,128,256]{2,1,0:T(8,128)S(1)} all-to-all(f32[8,128,256]{2,1,0:T(8,128)S(1)} %broadcast_in_dim.44), channel_id=1, replica_groups=mesh['y'=4,'z_high'=8,'z_low'=2,'inner'=2,'outer'=4] {'z_low','y'}, dimensions={0} | all-to-all | bytes 2097152 | tf_op jit(solution)/shard_map/all_to_all | solution.py:188
  184.6 1.0 fusion
  185.6 1.0 convolution_bitcast_fusion.1
  186.6 1.0 fusion.2
  187.7 14.9 %all_to_all.69 = f32[8,40,256]{2,1,0:T(8,128)S(1)} all-to-all(f32[8,40,256]{2,1,0:T(8,128)S(1)} %bitcast.42), channel_id=1, replica_groups=mesh['y'=4,'z_high'=8,'z_low'=2,'inner'=2,'outer'=4] {'inner','outer'}, dimensions={0} | all-to-all | bytes 655360 | tf_op jit(solution)/shard_map/all_to_all | solution.py:188
  202.6 11.0 %all_to_all.70 = f32[8,40,256]{2,1,0:T(8,128)} all-to-all(f32[8,40,256]{2,1,0:T(8,128)S(1)} %broadcast_in_dim.45), channel_id=1, replica_groups=mesh['y'=4,'z_high'=8,'z_low'=2,'inner'=2,'outer'=4] {'inner','outer'}, dimensions={0} | all-to-all | bytes 655360 | tf_op jit(solution)/shard_map/all_to_all | solution.py:188
  213.6 11.5 %results.1 = (f32[1024,256]{1,0:T(8,128)}, f32[256,128]{1,0:T(8,128)}) custom-call(f32[320,256]{1,0:T(8,128)} %bitcast.48, f32[1024,256]{1,0:T(8,128)} %bitcast.35), custom_call_target="tpu_custom_call" | custom-call | flops 2000000000 | bytes 524288 | tf_op jit(solution)/shard_map/results/pallas_call | solution.py:166
  (16 shorter events, 0.2 us)
Async XLA Ops:
  0.6 1.0 copy-start
  111.6 1.0 copy-start.2
  130.3 17.3 %all-to-all-start.7 = ((f32[8,16,256]{2,1,0:T(8,128)}), f32[8,16,256]{2,1,0:T(8,128)S(1)}, u32[]{:S(2)}, u32[]{:S(2)}) async-start(f32[8,16,256]{2,1,0:T(8,128)} %bitcast.8), calls=%async_computation.7 | async-start | bytes 262144 | tf_op jit(solution)/shard_map/all_to_all | solution.py:188
  184.6 2.0 copy-start.1
